TPU v7x, 32 devices: a whole 2x2x4 slice. The times are simulated.
32 devices in a mesh: traj: 8 (over z, core), amp: 4 (over y, x).
Axes of the slice: x: 2, y: 2, z: 4, core: 2. Of those that a mesh axis runs over, the one named last changes fastest.
Arguments:
- amplitudes: float32 [8, 2, 524288], P('traj', None, 'amp'), parts along dimension 0, may hold values from -6 to 6
- couplings: float32 [18], replicated, may hold values from 0.5 to 2
- fields: float32 [19], replicated, may hold values from 0.5 to 2
- decays: float32 [19], replicated, may hold values from 0.2 to 2
- channel: int32 [8], P('traj'), parts along dimension 0, may hold values from 0 to 19
Outputs:
- evolved_state: float32 [8, 2, 524288], P('traj', None, 'amp'), parts along dimension 0
There are 8 independent parts, one for each index of `traj`. A program takes and returns all parts, laid end to end along the dimension named above; an argument that names none is the same for every part. Nothing has to cross between parts.
Inputs may be any that keep to these rules, and one draw needn't show every extreme that they name: `channel`: the value 19 means that the trajectory does not jump.
All inputs are finite; a program needn't handle non-finite values.
Results may differ from a plain program's by a relative error of at most 0.0003.
Values sent between devices are 32-bit elements; how exact they have to be, the bound alone decides.
No kernel may reach another device: no remote copies, remote signals or barrier semaphores. Data moves between devices by JAX's collectives and lax.ppermute only.
A program may use at most 256 MiB of HBM per device.

v0:
```python
import jax
import jax.numpy as jnp
from jax import lax
from jax.sharding import PartitionSpec as P

SPINS = 19
KRYLOV = 8


time_step = 0.7
squarings = 8
taylor_order = 10
highest = lax.Precision.HIGHEST


def partner_2(value, axis, distance):
    mask = 2**distance
    pairs = [(source, source ^ mask) for source in range(lax.axis_size(axis))]
    return lax.ppermute(value, axis, pairs)


def flip_axis(tensor, axis_pos, bit_pos):
    old_shape = tensor.shape
    new_shape = (
        old_shape[:axis_pos]
        + (old_shape[axis_pos] >> bit_pos + 1, 2, 1 << bit_pos)
        + old_shape[axis_pos + 1 :]
    )
    return jnp.flip(tensor.reshape(new_shape), axis=axis_pos + 1).reshape(old_shape)


def krylov_weights(scale_norm, hess_real, hess_imag):
    a_real = time_step * hess_imag
    a_imag = -time_step * hess_real
    upper_half = jnp.concatenate([a_real, -a_imag], axis=2)
    lower_half = jnp.concatenate([a_imag, a_real], axis=2)
    scaled = jnp.concatenate([upper_half, lower_half], axis=1) / 2.0**squarings
    identity = jnp.broadcast_to(jnp.eye(2 * KRYLOV, dtype=jnp.float32), scaled.shape)
    series = identity
    for degree in range(taylor_order, 0, -1):
        series = identity + jnp.einsum("tij,tjk->tik", scaled, series, precision=highest) / degree
    for repeat in range(squarings):
        series = jnp.einsum("tij,tjk->tik", series, series, precision=highest)
    first_column = series[:, :, 0] * scale_norm[:, None]
    return (first_column[:, :KRYLOV], first_column[:, KRYLOV:])


def projections(local_proj):
    return lax.psum(local_proj, "amp")


def subtract_span(applied, stacked, projected):
    proj_real = projected[:, :, 0]
    proj_imag = projected[:, :, 1]
    comb_real = jnp.einsum(
        "tk,tkrl->trl", proj_real, stacked[:, :, 0], precision=highest
    ) - jnp.einsum("tk,tkrl->trl", proj_imag, stacked[:, :, 1], precision=highest)
    comb_imag = jnp.einsum(
        "tk,tkrl->trl", proj_real, stacked[:, :, 1], precision=highest
    ) + jnp.einsum("tk,tkrl->trl", proj_imag, stacked[:, :, 0], precision=highest)
    return applied - jnp.stack([comb_real, comb_imag], axis=1)


def body(amplitudes, couplings, fields, decays, channel):
    node_count = lax.axis_size("amp")
    high_bits = node_count.bit_length() - 1
    device = lax.axis_index("amp")
    traj_count = amplitudes.shape[0]
    local_len = amplitudes.shape[2]
    row_count = local_len // 128
    block_len = local_len // node_count
    low_spins = SPINS - high_bits
    band_low = SPINS - 2 * high_bits
    local_ids = jnp.arange(local_len, dtype=jnp.int32)
    position = device * local_len + local_ids
    occupation = [(position >> spin_pos & 1).astype(jnp.float32) for spin_pos in range(SPINS)]
    diag_real = jnp.zeros((local_len,), jnp.float32)
    for spin_pos in range(SPINS - 1):
        diag_real = diag_real - couplings[spin_pos] * (1.0 - 2.0 * occupation[spin_pos]) * (
            1.0 - 2.0 * occupation[spin_pos + 1]
        )
    diag_imag = jnp.zeros((local_len,), jnp.float32)
    for spin_pos in range(SPINS):
        diag_imag = diag_imag - 0.5 * decays[spin_pos] * occupation[spin_pos]
    diag_real = diag_real.reshape(row_count, 128)
    diag_imag = diag_imag.reshape(row_count, 128)
    lane_ids = jnp.arange(128, dtype=jnp.int32)
    crossed = lane_ids[:, None] ^ lane_ids[None, :]
    lane_table = jnp.zeros((128, 128), jnp.float32)
    for spin_pos in range(7):
        lane_table = lane_table + fields[spin_pos] * (crossed == 1 << spin_pos).astype(jnp.float32)
    vector = amplitudes.reshape(traj_count, 2, row_count, 128)
    start_sq = lax.psum(jnp.sum(vector * vector, axis=(1, 2, 3)), "amp")
    scale_norm = jnp.sqrt(start_sq)
    krylov_basis = [vector / scale_norm[:, None, None, None]]
    hess_real = jnp.zeros((traj_count, KRYLOV, KRYLOV), jnp.float32)
    hess_imag = jnp.zeros((traj_count, KRYLOV, KRYLOV), jnp.float32)
    for column in range(KRYLOV):
        apply_vector = krylov_basis[column]
        flipped = jnp.einsum("tcrl,lm->tcrm", apply_vector, lane_table, precision=highest)
        for apply_spin_pos in range(7, low_spins):
            flipped = flipped + fields[apply_spin_pos] * flip_axis(
                apply_vector, 2, apply_spin_pos - 7
            )
        for apply_bit_pos in range(high_bits):
            partner = partner_2(apply_vector, "amp", apply_bit_pos)
            flipped = flipped + fields[low_spins + apply_bit_pos] * partner
        real_part = apply_vector[:, 0]
        imag_part = apply_vector[:, 1]
        out_real = diag_real * real_part - diag_imag * imag_part - flipped[:, 0]
        out_imag = diag_real * imag_part + diag_imag * real_part - flipped[:, 1]
        applied = jnp.stack([out_real, out_imag], axis=1)
        stacked = jnp.stack(krylov_basis, axis=1)
        swapped = jnp.stack([applied[:, 1], -applied[:, 0]], axis=1)
        paired = jnp.stack([applied, swapped], axis=1)
        local_proj = jnp.einsum("tkcrl,tpcrl->tkp", stacked, paired, precision=highest)
        if column + 1 == KRYLOV:
            projected = projections(local_proj)
        else:
            local_sq = jnp.sum(applied * applied, axis=(1, 2, 3))
            projected, whole_sq = lax.psum((local_proj, local_sq), "amp")
            residual = subtract_span(applied, stacked, projected)
            squares = whole_sq - jnp.sum(projected * projected, axis=(1, 2))
            column_norm = jnp.sqrt(squares)
            hess_real = hess_real.at[:, column + 1, column].set(column_norm)
            krylov_basis.append(residual / column_norm[:, None, None, None])
        hess_real = hess_real.at[:, : column + 1, column].set(projected[:, :, 0])
        hess_imag = hess_imag.at[:, : column + 1, column].set(projected[:, :, 1])
    weights_real, weights_imag = krylov_weights(scale_norm, hess_real, hess_imag)
    stacked = jnp.stack(krylov_basis, axis=1)
    new_real = jnp.einsum(
        "tk,tkrl->trl", weights_real, stacked[:, :, 0], precision=highest
    ) - jnp.einsum("tk,tkrl->trl", weights_imag, stacked[:, :, 1], precision=highest)
    new_imag = jnp.einsum(
        "tk,tkrl->trl", weights_real, stacked[:, :, 1], precision=highest
    ) + jnp.einsum("tk,tkrl->trl", weights_imag, stacked[:, :, 0], precision=highest)
    propagated = jnp.stack([new_real, new_imag], axis=1)
    lowered_local = jnp.zeros_like(propagated)
    for spin_pos in range(band_low, low_spins):
        vacant = (local_ids >> spin_pos & 1 == 0).reshape(row_count, 128)
        lowered_term = jnp.where(vacant, flip_axis(propagated, 2, spin_pos - 7), 0.0)
        lowered_local = jnp.where(
            (channel == spin_pos)[:, None, None, None], lowered_term, lowered_local
        )
    spread = propagated.reshape(traj_count, 2, node_count, block_len)
    relaid = lax.all_to_all(spread, "amp", split_axis=2, concat_axis=2, tiled=True)
    sources = jnp.arange(node_count, dtype=jnp.int32)
    offsets = jnp.arange(block_len, dtype=jnp.int32)
    lowered_relaid = jnp.zeros_like(relaid)
    for spin_pos in range(band_low):
        vacant = offsets >> spin_pos & 1 == 0
        lowered_term = jnp.where(vacant, flip_axis(relaid, 3, spin_pos), 0.0)
        lowered_relaid = jnp.where(
            (channel == spin_pos)[:, None, None, None], lowered_term, lowered_relaid
        )
    for bit_pos in range(high_bits):
        vacant = sources >> bit_pos & 1 == 0
        lowered_term = jnp.where(vacant[:, None], flip_axis(relaid, 2, bit_pos), 0.0)
        lowered_relaid = jnp.where(
            (channel == low_spins + bit_pos)[:, None, None, None], lowered_term, lowered_relaid
        )
    returned = lax.all_to_all(
        lowered_relaid, "amp", split_axis=2, concat_axis=2, tiled=True
    ).reshape(propagated.shape)
    in_band = (channel >= band_low) & (channel < low_spins)
    lowered = jnp.where(in_band[:, None, None, None], lowered_local, returned)
    jumped = channel < SPINS
    squared_sum = lax.psum(jnp.sum(lowered * lowered, axis=(1, 2, 3)), "amp")
    squared_sum = jnp.where(jumped, squared_sum, jnp.float32(local_len * node_count))
    lowered = lowered * jnp.sqrt(local_len * node_count / squared_sum)[:, None, None, None]
    result = jnp.where(jumped[:, None, None, None], lowered, propagated)
    return result.reshape(traj_count, 2, local_len)


def solution(mesh):
    placed = (P("traj", None, "amp"), P(), P(), P(), P("traj"))
    return jax.shard_map(
        body, mesh=mesh, in_specs=placed, out_specs=P("traj", None, "amp"), check_vma=False
    )
```

profile of v0, /device:TPU:0, one launch (start us, length us, event | category | flops | bytes accessed | tf_op | source)
XLA Modules:
  0.0 2174.6 jit_solution(13857305890439002905)
XLA Ops:
  193.2 15.8 slice_subtract_fusion.12
  209.0 15.7 fusion.377
  231.1 20.7 convolution_bitcast_fusion.7
  368.7 15.7 fusion.376
  390.9 21.1 convolution_bitcast_fusion.6
  532.7 15.7 fusion.375
  551.8 21.2 convolution_bitcast_fusion.5
  712.8 21.3 convolution_bitcast_fusion.4
  878.2 21.5 convolution_bitcast_fusion.3
  1044.3 21.7 convolution_bitcast_fusion.2
  1209.7 20.6 convolution_bitcast_fusion.1
  1296.1 66.1 %reshape.8754 = f32[1,2,4,4096,2,4]{5,4,3,2,1,0:T(2,128)} reshape(f32[1,2,4,32768]{3,2,1,0:T(4,128)S(1)} %copy.136) | data formatting | bytes 2097152 | tf_op jit(solution)/shard_map/reshape | solution.py:29
  1362.2 32.7 %reshape.8752 = f32[1,2,4,2048,2,8]{5,4,3,2,1,0:T(2,128)} reshape(f32[1,2,4,32768]{3,2,1,0:T(4,128)S(1)} %copy.136) | data formatting | bytes 2097152 | tf_op jit(solution)/shard_map/reshape | solution.py:29
  1417.9 16.4 copy.141
  1434.3 156.0 %rev.422 = f32[1,2,4,16384,2,1]{2,4,3,1,5,0:T(2,128)} reverse(f32[1,2,4,16384,2,1]{2,4,3,1,5,0:T(2,128)} %bitcast.1047), dimensions={4} | reverse | bytes 2097152 | tf_op jit(solution)/shard_map/jit(_flip)/rev | solution.py:29
  1590.2 18.3 copy.144
  1608.5 23.3 %rev.421 = f32[1,2,4,8192,2,2]{2,5,4,3,1,0:T(2,128)} reverse(f32[1,2,4,8192,2,2]{2,5,4,3,1,0:T(2,128)} %bitcast.1048), dimensions={4} | reverse | bytes 2097152 | tf_op jit(solution)/shard_map/jit(_flip)/rev | solution.py:29
  1631.8 18.3 copy.142
  1650.1 155.9 %rev.420 = f32[1,2,4,4096,2,4]{5,4,3,2,1,0:T(2,128)} reverse(f32[1,2,4,4096,2,4]{5,4,3,2,1,0:T(2,128)} %reshape.8754), dimensions={4} | reverse | bytes 2097152 | tf_op jit(solution)/shard_map/jit(_flip)/rev | solution.py:29
  1806.0 62.0 %reshape.8755 = f32[1,2,4,32768]{3,2,1,0:T(4,128)} reshape(f32[1,2,4,4096,2,4]{5,4,3,2,1,0:T(2,128)} %rev.420) | data formatting | bytes 2097152 | tf_op jit(solution)/shard_map/reshape | solution.py:29
  1868.0 78.5 %rev.419 = f32[1,2,4,2048,2,8]{5,4,3,2,1,0:T(2,128)} reverse(f32[1,2,4,2048,2,8]{5,4,3,2,1,0:T(2,128)} %reshape.8752), dimensions={4} | reverse | bytes 2097152 | tf_op jit(solution)/shard_map/jit(_flip)/rev | solution.py:29
  1946.5 35.0 %reshape.8753 = f32[1,2,4,32768]{3,2,1,0:T(4,128)} reshape(f32[1,2,4,2048,2,8]{5,4,3,2,1,0:T(2,128)} %rev.419) | data formatting | bytes 2097152 | tf_op jit(solution)/shard_map/reshape | solution.py:29
  1981.5 39.9 %rev.418 = f32[1,2,4,1024,2,16]{5,4,3,2,1,0:T(2,128)} reverse(f32[1,2,4,1024,2,16]{5,4,3,2,1,0:T(2,128)} %reshape.8750), dimensions={4} | reverse | bytes 2097152 | tf_op jit(solution)/shard_map/jit(_flip)/rev | solution.py:29
  2035.6 20.6 rev.417
  (675 shorter events, 1215.1 us)
Async XLA Ops:
  17.3 61.5 %collective-permute-start.1 = (f32[1,2,1024,128]{3,2,1,0:T(8,128)S(1)}, f32[1,2,1024,128]{3,2,1,0:T(8,128)}, u32[]{:S(2)}, u32[]{:S(2)}) collective-permute-start(f32[1,2,1024,128]{3,2,1,0:T(8,128)S(1)} %copy.306), channel_id=1, source_target_pairs={{0,2},{1,3},{2,0},{3,1},{4,6},{5,7},{6,4},{7,5},{8,10},{9,11},{10,... | collective-permute-start | bytes 3145736 | tf_op jit(solution)/shard_map/ppermute | solution.py:19
  17.9 60.9 %collective-permute-start = (f32[1,2,1024,128]{3,2,1,0:T(8,128)S(1)}, f32[1,2,1024,128]{3,2,1,0:T(8,128)}, u32[]{:S(2)}, u32[]{:S(2)}) collective-permute-start(f32[1,2,1024,128]{3,2,1,0:T(8,128)S(1)} %copy.306), channel_id=1, source_target_pairs={{0,1},{1,0},{2,3},{3,2},{4,5},{5,4},{6,7},{7,6},{8,9},{9,8},{10,11... | collective-permute-start | bytes 3145736 | tf_op jit(solution)/shard_map/ppermute | solution.py:19
  22.9 21.1 copy-start.85
  22.9 22.4 %copy-start.84 = (s32[3]{0:T(128)S(1)}, s32[3]{0:T(128)}, u32[]{:S(2)}) copy-start(s32[3]{0:T(128)} %constant.807.clone.1) | copy-start | bytes 40
  58.8 20.0 copy-start.18
  136.9 53.3 %collective-permute-start.3 = (f32[1,2,1024,128]{3,2,1,0:T(8,128)}, f32[1,2,1024,128]{3,2,1,0:T(8,128)}, u32[]{:S(2)}, u32[]{:S(2)}) collective-permute-start(f32[1,2,1024,128]{3,2,1,0:T(8,128)} %fusion.146), channel_id=1, source_target_pairs={{0,2},{1,3},{2,0},{3,1},{4,6},{5,7},{6,4},{7,5},{8,10},{9,11},{10,... | collective-permute-start | bytes 3145736 | tf_op jit(solution)/shard_map/ppermute | solution.py:19
  137.5 52.7 %collective-permute-start.2 = (f32[1,2,1024,128]{3,2,1,0:T(8,128)}, f32[1,2,1024,128]{3,2,1,0:T(8,128)}, u32[]{:S(2)}, u32[]{:S(2)}) collective-permute-start(f32[1,2,1024,128]{3,2,1,0:T(8,128)} %fusion.146), channel_id=1, source_target_pairs={{0,1},{1,0},{2,3},{3,2},{4,5},{5,4},{6,7},{7,6},{8,9},{9,8},{10,11... | collective-permute-start | bytes 3145736 | tf_op jit(solution)/shard_map/ppermute | solution.py:19
  231.1 32.7 %copy-start.64 = (f32[2,1024,128]{2,1,0:T(8,128)S(1)}, f32[2,1024,128]{2,1,0:T(8,128)}, u32[]{:S(2)}) copy-start(f32[2,1024,128]{2,1,0:T(8,128)} %get-tuple-element.352) | copy-start | bytes 3145732
  291.2 58.9 %collective-permute-start.5 = (f32[1,2,1024,128]{3,2,1,0:T(8,128)}, f32[1,2,1024,128]{3,2,1,0:T(8,128)}, u32[]{:S(2)}, u32[]{:S(2)}) collective-permute-start(f32[1,2,1024,128]{3,2,1,0:T(8,128)} %fusion.155), channel_id=1, source_target_pairs={{0,2},{1,3},{2,0},{3,1},{4,6},{5,7},{6,4},{7,5},{8,10},{9,11},{10,... | collective-permute-start | bytes 3145736 | tf_op jit(solution)/shard_map/ppermute | solution.py:19
  291.8 58.3 %collective-permute-start.4 = (f32[1,2,1024,128]{3,2,1,0:T(8,128)}, f32[1,2,1024,128]{3,2,1,0:T(8,128)}, u32[]{:S(2)}, u32[]{:S(2)}) collective-permute-start(f32[1,2,1024,128]{3,2,1,0:T(8,128)} %fusion.155), channel_id=1, source_target_pairs={{0,1},{1,0},{2,3},{3,2},{4,5},{5,4},{6,7},{7,6},{8,9},{9,8},{10,11... | collective-permute-start | bytes 3145736 | tf_op jit(solution)/shard_map/ppermute | solution.py:19
  425.4 22.3 %copy-start.13 = (f32[3,1024,128]{2,1,0:T(8,128)S(1)}, f32[3,1024,128]{2,1,0:T(8,128)}, u32[]{:S(2)}) copy-start(f32[3,1024,128]{2,1,0:T(8,128)} %get-tuple-element.346) | copy-start | bytes 4718596
  456.3 57.9 %collective-permute-start.7 = (f32[1,2,1024,128]{3,2,1,0:T(8,128)}, f32[1,2,1024,128]{3,2,1,0:T(8,128)}, u32[]{:S(2)}, u32[]{:S(2)}) collective-permute-start(f32[1,2,1024,128]{3,2,1,0:T(8,128)} %fusion.164), channel_id=1, source_target_pairs={{0,2},{1,3},{2,0},{3,1},{4,6},{5,7},{6,4},{7,5},{8,10},{9,11},{10,... | collective-permute-start | bytes 3145736 | tf_op jit(solution)/shard_map/ppermute | solution.py:19
  456.9 57.3 %collective-permute-start.6 = (f32[1,2,1024,128]{3,2,1,0:T(8,128)}, f32[1,2,1024,128]{3,2,1,0:T(8,128)}, u32[]{:S(2)}, u32[]{:S(2)}) collective-permute-start(f32[1,2,1024,128]{3,2,1,0:T(8,128)} %fusion.164), channel_id=1, source_target_pairs={{0,1},{1,0},{2,3},{3,2},{4,5},{5,4},{6,7},{7,6},{8,9},{9,8},{10,11... | collective-permute-start | bytes 3145736 | tf_op jit(solution)/shard_map/ppermute | solution.py:19
  551.8 36.7 %copy-start.15 = (f32[4,1024,128]{2,1,0:T(8,128)S(1)}, f32[4,1024,128]{2,1,0:T(8,128)}, u32[]{:S(2)}) copy-start(f32[4,1024,128]{2,1,0:T(8,128)} %get-tuple-element.342) | copy-start | bytes 6291460
  618.2 56.9 %collective-permute-start.9 = (f32[1,2,1024,128]{3,2,1,0:T(8,128)S(1)}, f32[1,2,1024,128]{3,2,1,0:T(8,128)}, u32[]{:S(2)}, u32[]{:S(2)}) collective-permute-start(f32[1,2,1024,128]{3,2,1,0:T(8,128)S(1)} %fusion.173), channel_id=1, source_target_pairs={{0,2},{1,3},{2,0},{3,1},{4,6},{5,7},{6,4},{7,5},{8,10},{9,11},{10,... | collective-permute-start | bytes 3145736 | tf_op jit(solution)/shard_map/ppermute | solution.py:19
  618.9 56.3 %collective-permute-start.8 = (f32[1,2,1024,128]{3,2,1,0:T(8,128)S(1)}, f32[1,2,1024,128]{3,2,1,0:T(8,128)}, u32[]{:S(2)}, u32[]{:S(2)}) collective-permute-start(f32[1,2,1024,128]{3,2,1,0:T(8,128)S(1)} %fusion.173), channel_id=1, source_target_pairs={{0,1},{1,0},{2,3},{3,2},{4,5},{5,4},{6,7},{7,6},{8,9},{9,8},{10,11... | collective-permute-start | bytes 3145736 | tf_op jit(solution)/shard_map/ppermute | solution.py:19
  782.9 57.8 %collective-permute-start.11 = (f32[1,2,1024,128]{3,2,1,0:T(8,128)S(1)}, f32[1,2,1024,128]{3,2,1,0:T(8,128)}, u32[]{:S(2)}, u32[]{:S(2)}) collective-permute-start(f32[1,2,1024,128]{3,2,1,0:T(8,128)S(1)} %fusion.182), channel_id=1, source_target_pairs={{0,2},{1,3},{2,0},{3,1},{4,6},{5,7},{6,4},{7,5},{8,10},{9,11},{10,... | collective-permute-start | bytes 3145736 | tf_op jit(solution)/shard_map/ppermute | solution.py:19
  783.5 57.1 %collective-permute-start.10 = (f32[1,2,1024,128]{3,2,1,0:T(8,128)S(1)}, f32[1,2,1024,128]{3,2,1,0:T(8,128)}, u32[]{:S(2)}, u32[]{:S(2)}) collective-permute-start(f32[1,2,1024,128]{3,2,1,0:T(8,128)S(1)} %fusion.182), channel_id=1, source_target_pairs={{0,1},{1,0},{2,3},{3,2},{4,5},{5,4},{6,7},{7,6},{8,9},{9,8},{10,11... | collective-permute-start | bytes 3145736 | tf_op jit(solution)/shard_map/ppermute | solution.py:19
  949.4 57.5 %collective-permute-start.13 = (f32[1,2,1024,128]{3,2,1,0:T(8,128)S(1)}, f32[1,2,1024,128]{3,2,1,0:T(8,128)}, u32[]{:S(2)}, u32[]{:S(2)}) collective-permute-start(f32[1,2,1024,128]{3,2,1,0:T(8,128)S(1)} %fusion.191), channel_id=1, source_target_pairs={{0,2},{1,3},{2,0},{3,1},{4,6},{5,7},{6,4},{7,5},{8,10},{9,11},{10,... | collective-permute-start | bytes 3145736 | tf_op jit(solution)/shard_map/ppermute | solution.py:19
  950.0 56.9 %collective-permute-start.12 = (f32[1,2,1024,128]{3,2,1,0:T(8,128)S(1)}, f32[1,2,1024,128]{3,2,1,0:T(8,128)}, u32[]{:S(2)}, u32[]{:S(2)}) collective-permute-start(f32[1,2,1024,128]{3,2,1,0:T(8,128)S(1)} %fusion.191), channel_id=1, source_target_pairs={{0,1},{1,0},{2,3},{3,2},{4,5},{5,4},{6,7},{7,6},{8,9},{9,8},{10,11... | collective-permute-start | bytes 3145736 | tf_op jit(solution)/shard_map/ppermute | solution.py:19
  1116.0 57.0 %collective-permute-start.15 = (f32[1,2,1024,128]{3,2,1,0:T(8,128)S(1)}, f32[1,2,1024,128]{3,2,1,0:T(8,128)}, u32[]{:S(2)}, u32[]{:S(2)}) collective-permute-start(f32[1,2,1024,128]{3,2,1,0:T(8,128)S(1)} %fusion.201), channel_id=1, source_target_pairs={{0,2},{1,3},{2,0},{3,1},{4,6},{5,7},{6,4},{7,5},{8,10},{9,11},{10,... | collective-permute-start | bytes 3145736 | tf_op jit(solution)/shard_map/ppermute | solution.py:19
  1116.6 56.4 %collective-permute-start.14 = (f32[1,2,1024,128]{3,2,1,0:T(8,128)S(1)}, f32[1,2,1024,128]{3,2,1,0:T(8,128)}, u32[]{:S(2)}, u32[]{:S(2)}) collective-permute-start(f32[1,2,1024,128]{3,2,1,0:T(8,128)S(1)} %fusion.201), channel_id=1, source_target_pairs={{0,1},{1,0},{2,3},{3,2},{4,5},{5,4},{6,7},{7,6},{8,9},{9,8},{10,11... | collective-permute-start | bytes 3145736 | tf_op jit(solution)/shard_map/ppermute | solution.py:19
  1282.3 13.1 all-to-all-start
  2139.4 15.6 all-to-all-start.1
  (85 other events, 699.6 us)
where the time goes:
time: 2200 us; the launch traced here: 2170 us
  local copies, waits for them, and re-layouts  1050 us (48%)
  other arithmetic  535 us (24%)
  matrix products  433 us (20%)
  blocking collectives  110 us (5%)
  between operations  25.7 us (1%)
    rev x19, local copies, waits for them, and re-layouts, flip_axis(): jnp.flip(tensor.reshape(new_shape), axis=axis_pos + 1).reshape(old_shape)  514 us
    reshape x19, local copies, waits for them, and re-layouts, flip_axis(): jnp.flip(tensor.reshape(new_shape), axis=axis_pos + 1).reshape(old_shape)  180 us
    another operation x35, local copies, waits for them, and re-layouts  154 us
    mul x80, other arithmetic, body(): fields[apply_spin_pos] * flip_axis(apply_vector, 2, apply_spin_pos - 7)  150 us
    dot_general x7, matrix products, body(): jnp.einsum('tkcrl,tpcrl->tkp', stacked, paired, precision=highest)  148 us
    reshape x21, local copies, waits for them, and re-layouts, flip_axis(): tensor.reshape(new_shape)  131 us
    sub x8, other arithmetic, body(): out_imag = diag_real * imag_part + diag_imag * real_part - flipped[:, 1]  120 us
    neg x8, other arithmetic, body(): swapped = jnp.stack([applied[:, 1], -applied[:, 0]], axis=1)  120 us
  transfers between devices with their start and end apart: 18, of which 1 were waited for; matrix products, arithmetic and copies ran while one was open for 21% of the time, Pallas kernels for 0%

commit v1 on v0

v1 whole, which is shorter than its diff:
```python
import functools
import jax
import jax.numpy as jnp
from jax import lax
from jax.experimental import pallas as pl
from jax.experimental.pallas import tpu as pltpu
from jax.sharding import PartitionSpec as P

KRYLOV = 8
time_step = 0.7
squarings = 8
taylor_order = 10
highest = lax.Precision.HIGHEST
LANES = 128
TILE = (8, LANES)
BLOCK = 256
CHUNK = 2 * BLOCK


def partner(value, mask):
    count = lax.axis_size("amp")
    return lax.ppermute(value, "amp", [(i, i ^ mask) for i in range(count)])


def gather_state(own, high_bits):
    rows = own.shape[2] // LANES
    if high_bits == 2:
        half = own.shape[2] // 2
        first = partner(own, 1)
        second = partner(own, 2)
        third_low = partner(first[:, :, :half], 2)
        third_high = partner(second[:, :, half:], 1)
        return [
            (0, own),
            (rows, first),
            (2 * rows, second),
            (3 * rows, third_low),
            (3 * rows + rows // 2, third_high),
        ]
    pieces = [(0, own)]
    for bit in range(high_bits):
        pieces += [(start + (rows << bit), partner(piece, 1 << bit)) for start, piece in pieces]
    return pieces


def interleaved(piece):
    rows = piece.shape[2] // LANES
    return piece.reshape(2, rows, LANES).transpose(1, 0, 2).reshape(2 * rows, LANES)


def splat(value):
    return jnp.broadcast_to(value, TILE)


def total(acc):
    return splat(jnp.sum(acc, keepdims=True))


def cmul(a, b):
    return (a[0] * b[0] - a[1] * b[1], a[0] * b[1] + a[1] * b[0])


def conj(a):
    return (a[0], -a[1])


def sub(a, b):
    return (a[0] - b[0], a[1] - b[1])


def scale(a, r):
    return (a[0] * r, a[1] * r)


def kernel(spins, starts, *refs):
    count = len(starts)
    fields, row_real, row_imag, channel, device = refs[:5]
    low_real, low_imag, mats = refs[5:8]
    pieces = refs[8 : 8 + count]
    out = refs[8 + count]
    basis_r, basis_i, high, low, table = refs[9 + count :]
    rows_total = basis_r.shape[1]
    groups = rows_total // 8
    rows_out = out.shape[0] // 2
    zero = jnp.zeros(TILE, jnp.float32)

    norm = zero
    for start, piece in zip(starts, pieces):

        def take(g, acc, start=start, piece=piece):
            re = piece[pl.ds(pl.multiple_of(g * 16, 16), 8, stride=2), :]
            im = piece[pl.ds(g * 16 + 1, 8, stride=2), :]
            row = pl.multiple_of(start + g * 8, 8)
            basis_r[0, pl.ds(row, 8), :] = re
            basis_i[0, pl.ds(row, 8), :] = im
            return acc + (re * re + im * im)

        norm = lax.fori_loop(0, piece.shape[0] // 16, take, norm, unroll=8)

    def product(part, block, slot, row):
        xh = high[2 * part + block]
        xl = low[2 * part + block]
        return xh, xl

    def chunk_flips(c, slot):
        left_h, left_l, right_h, right_l = mats[0], mats[1], mats[2], mats[3]
        base = pl.multiple_of(c * CHUNK, CHUNK)
        for part, ref in ((0, basis_r), (1, basis_i)):
            xh, xl = high[part], low[part]
            dot = functools.partial(jnp.dot, preferred_element_type=jnp.float32)
            y = dot(left_h, xh) + dot(left_l, xh) + dot(left_h, xl)
            y = y + dot(xh, right_h) + dot(xh, right_l) + dot(xl, right_h)
            ref[slot, pl.ds(base, BLOCK), :] = y[:, :LANES]
            ref[slot, pl.ds(base + BLOCK, BLOCK), :] = y[:, LANES:]

    def halves(part, block, r, value):
        h = value.astype(jnp.bfloat16)
        l = (value - h.astype(jnp.float32)).astype(jnp.bfloat16)
        high[part, pl.ds(r, 16), pl.ds(block * LANES, LANES)] = h
        low[part, pl.ds(r, 16), pl.ds(block * LANES, LANES)] = l

    gram = {}
    diag_a, real_b, norms = [], [], [total(norm)]
    gram[0, 0] = (norms[0], zero)
    inner = None
    scale0 = lax.rsqrt(norms[0])
    for step in range(KRYLOV):
        def make(c, acc, step=step):
            base = pl.multiple_of(c * CHUNK, CHUNK)
            for block in range(2):
                for r in range(0, BLOCK, 16):
                    at = pl.ds(base + block * BLOCK + r, 16)
                    re = basis_r[step, at, :]
                    im = basis_i[step, at, :]
                    if step > 0:
                        pr, pi = basis_r[step - 1, at, :], basis_i[step - 1, at, :]
                        ar = jnp.concatenate([diag_a[step - 1][0]] * 2)
                        ai = jnp.concatenate([diag_a[step - 1][1]] * 2)
                        if step == 1:
                            s = jnp.concatenate([scale0] * 2)
                            re, im = re * s, im * s
                        re = re - (ar * pr - ai * pi)
                        im = im - (ar * pi + ai * pr)
                        if step > 1:
                            b = jnp.concatenate([real_b[step - 1]] * 2)
                            re = re - b * basis_r[step - 2, at, :]
                            im = im - b * basis_i[step - 2, at, :]
                        basis_r[step, at, :] = re
                        basis_i[step, at, :] = im
                        sq = re * re + im * im
                        acc = acc + (sq[:8] + sq[8:])
                    halves(0, block, r, re)
                    halves(1, block, r, im)
            chunk_flips(c, step + 1)
            return acc

        square = lax.fori_loop(0, rows_total // CHUNK, make, zero)
        if step > 0:
            square = total(square)
            gram[step, step] = (square, zero)
            norms.append(square)

        far = [(b, fields[7 + b]) for b in range(9, spins - 7)]
        lr, li = (low_real[0], low_real[1]), low_imag[...]

        def apply(c, accs, step=step):
            accs = list(accs)
            base = pl.multiple_of(c * 64, 64)
            for r in range(8):
                at = pl.ds(pl.multiple_of(base + 8 * r, 8), 8)
                xr, xi = basis_r[step, at, :], basis_i[step, at, :]
                wr, wi = basis_r[step + 1, at, :], basis_i[step + 1, at, :]
                for bit, weight in far:
                    other = pl.ds(pl.multiple_of((base ^ (1 << bit)) + 8 * r, 8), 8)
                    wr = wr - weight * basis_r[step, other, :]
                    wi = wi - weight * basis_i[step, other, :]
                dr = lr[r & 1] + row_real[c * 8 + r]
                di = li + row_imag[c * 8 + r]
                wr = wr + (dr * xr - di * xi)
                wi = wi + (dr * xi + di * xr)
                if step + 1 < KRYLOV:
                    basis_r[step + 1, at, :] = wr
                    basis_i[step + 1, at, :] = wi
                for k in range(step + 1):
                    ur, ui = (xr, xi) if k == step else (basis_r[k, at, :], basis_i[k, at, :])
                    accs[2 * k] = accs[2 * k] + (ur * wr + ui * wi)
                    accs[2 * k + 1] = accs[2 * k + 1] + (ur * wi - ui * wr)
            return tuple(accs)

        sums = lax.fori_loop(0, groups // 8, apply, (zero,) * (2 * step + 2))
        inner = [(total(sums[2 * k]), total(sums[2 * k + 1])) for k in range(step + 1)]
        inverse = 1.0 / norms[step]
        unit = scale0 if step == 0 else jnp.ones(TILE, jnp.float32)
        inner = [scale(x, unit) for x in inner] if step == 0 else inner
        diag_a.append(scale(inner[step], inverse))
        real_b.append(inner[step - 1][0] / norms[step - 1] if step > 0 else zero)
        if step + 1 < KRYLOV:
            for k in range(step + 1):
                g = lambda i, j: gram[i, j] if i <= j else conj(gram[j, i])
                value = sub(inner[k], cmul(diag_a[step], g(k, step)))
                if step > 0:
                    value = sub(value, scale(g(k, step - 1), real_b[step]))
                gram[k, step + 1] = value

    size = [jnp.sqrt(x) for x in norms]
    inv = [1.0 / x for x in size]
    mat = {}
    for j in range(KRYLOV):
        for k in range(j + 1):
            mat[j, k] = conj(scale(gram[k, j], inv[k] * inv[j]))
    rhs = [scale(inner[k], inv[k] * inv[KRYLOV - 1]) for k in range(KRYLOV)]
    factor, pivot = {}, []
    for j in range(KRYLOV):
        d = mat[j, j][0]
        for k in range(j):
            d = d - (factor[j, k][0] * factor[j, k][0] + factor[j, k][1] * factor[j, k][1]) * pivot[k]
        pivot.append(d)
        r = 1.0 / d
        for i in range(j + 1, KRYLOV):
            x = mat[i, j]
            for k in range(j):
                x = sub(x, scale(cmul(factor[i, k], conj(factor[j, k])), pivot[k]))
            factor[i, j] = scale(x, r)
    last = list(rhs)
    for i in range(KRYLOV):
        for k in range(i):
            last[i] = sub(last[i], cmul(factor[i, k], last[k]))
    last = [scale(x, 1.0 / pivot[i]) for i, x in enumerate(last)]
    for i in reversed(range(KRYLOV)):
        for k in range(i + 1, KRYLOV):
            last[i] = sub(last[i], cmul(conj(factor[k, i]), last[k]))

    entries = {}
    for j in range(KRYLOV - 1):
        entries[j, j] = diag_a[j] if j > 0 else scale(diag_a[0], size[0])
        grow = size[1] if j == 0 else size[j + 1] * inv[j]
        entries[j + 1, j] = (grow, zero)
        if j > 0:
            entries[j - 1, j] = (real_b[j] * (size[j - 1] * inv[j]), zero)
    for i in range(KRYLOV):
        entries[i, KRYLOV - 1] = last[i]
    order = 2 * KRYLOV
    row_id = lax.broadcasted_iota(jnp.int32, (LANES, LANES), 0)
    col_id = lax.broadcasted_iota(jnp.int32, (LANES, LANES), 1)
    code = lax.broadcasted_iota(jnp.int32, TILE, 0) * LANES + lax.broadcasted_iota(jnp.int32, TILE, 1)
    quads = [[zero, zero], [zero, zero]]
    for (i, j), (re, im) in entries.items():
        here = code == i * LANES + j
        there = code == i * LANES + j + KRYLOV
        ar, ai = time_step * im, -time_step * re
        quads[0][0] = jnp.where(here, ar, jnp.where(there, -ai, quads[0][0]))
        quads[1][0] = jnp.where(here, ai, jnp.where(there, ar, quads[1][0]))
    table[...] = jnp.zeros_like(table)
    table[0:8, :] = quads[0][0] * (1.0 / 2.0**squarings)
    table[8:16, :] = quads[1][0] * (1.0 / 2.0**squarings)
    one = table[...]
    eye = jnp.where((row_id == col_id) & (row_id < order), 1.0, 0.0)
    times = functools.partial(jnp.dot, precision=highest, preferred_element_type=jnp.float32)
    two = times(one, one)
    three = times(two, one)
    f = [1.0]
    for d in range(1, taylor_order + 1):
        f.append(f[-1] / d)
    series = f[9] * eye + f[10] * one
    for d in (6, 3, 0):
        series = (f[d] * eye + f[d + 1] * one + f[d + 2] * two) + times(three, series)
    for repeat in range(squarings):
        series = times(series, series)
    table[...] = series
    weights = []
    for k in range(KRYLOV):
        c = size[0] * inv[k]
        weights.append((splat(table[k : k + 1, 0:1]) * c, splat(table[k + 8 : k + 9, 0:1]) * c))

    jump = channel[0]
    first = device[0]
    lane = lax.broadcasted_iota(jnp.int32, TILE, 1)
    sublane = lax.broadcasted_iota(jnp.int32, TILE, 0)
    inside = sublane * LANES + lane
    far_jump = jump >= 10
    low_bit = jnp.where(far_jump, 0, jump)
    high_bit = jnp.where(far_jump, jump - 10, 0)
    set_low = ((inside >> low_bit) & 1) == 1
    groups_out = rows_out // 8
    absolute = first * groups_out

    def combine(c, acc):
        for r in range(4):
            g = c * 4 + r
            at = pl.ds(pl.multiple_of(g * 8, 8), 8)
            pr, pi = zero, zero
            for k in range(KRYLOV):
                cr, ci = weights[k]
                ur, ui = basis_r[k, at, :], basis_i[k, at, :]
                pr = pr + (cr * ur - ci * ui)
                pi = pi + (cr * ui + ci * ur)
            basis_r[KRYLOV, at, :] = pr
            basis_i[KRYLOV, at, :] = pi
            raised = jnp.where(far_jump, ((g ^ absolute) >> high_bit) & 1, 1)
            acc = acc + raised.astype(jnp.float32) * (pr * pr + pi * pi)
        return acc

    weight = lax.fori_loop(0, groups // 4, combine, zero)
    weight = total(jnp.where(set_low | far_jump, weight, 0.0))
    gain = jnp.sqrt((rows_total * LANES) / weight)

    def put(g, re, im):
        out[pl.ds(pl.multiple_of(g * 16, 16), 8, stride=2), :] = re
        out[pl.ds(g * 16 + 1, 8, stride=2), :] = im

    def stay(g, _):
        at = pl.ds(pl.multiple_of(g * 8, 8), 8)
        put(g, basis_r[KRYLOV, at, :], basis_i[KRYLOV, at, :])
        return 0

    def lower_far(g, _):
        at = pl.ds(pl.multiple_of((g ^ (1 << high_bit)) * 8, 8), 8)
        vacant = 1 - (((g ^ absolute) >> high_bit) & 1)
        factor = gain * vacant.astype(jnp.float32)
        put(g, factor * basis_r[KRYLOV, at, :], factor * basis_i[KRYLOV, at, :])
        return 0

    def lower_lane(g, _):
        at = pl.ds(pl.multiple_of(g * 8, 8), 8)
        shift = LANES - (1 << low_bit)
        factor = jnp.where(set_low, 0.0, gain)
        put(
            g,
            factor * pltpu.roll(basis_r[KRYLOV, at, :], shift, 1),
            factor * pltpu.roll(basis_i[KRYLOV, at, :], shift, 1),
        )
        return 0

    def lower_sublane(bit):
        def run(g, _):
            at = pl.ds(pl.multiple_of(g * 8, 8), 8)
            shift = 8 - (1 << bit)
            factor = jnp.where(set_low, 0.0, gain)
            put(
                g,
                factor * pltpu.roll(basis_r[KRYLOV, at, :], shift, 0),
                factor * pltpu.roll(basis_i[KRYLOV, at, :], shift, 0),
            )
            return 0

        return run

    def over_output(run):
        lax.fori_loop(0, groups_out, run, 0, unroll=4)

    pl.when(jump == spins)(lambda: over_output(stay))
    pl.when((jump >= 10) & (jump < spins))(lambda: over_output(lower_far))
    pl.when(jump < 7)(lambda: over_output(lower_lane))
    for bit in range(3):
        pl.when(jump == 7 + bit)(functools.partial(over_output, lower_sublane(bit)))


def body(amplitudes, couplings, fields, decays, channel):
    node_count = lax.axis_size("amp")
    high_bits = node_count.bit_length() - 1
    device = lax.axis_index("amp")
    local_len = amplitudes.shape[2]
    spins = fields.shape[0]
    rows_total = node_count * local_len // LANES
    groups = rows_total // 8
    pieces = gather_state(amplitudes, high_bits)

    tile_ids = jnp.arange(8 * LANES, dtype=jnp.int32).reshape(TILE)
    group_ids = jnp.arange(groups, dtype=jnp.int32) ^ (device * (local_len // LANES // 8))
    bits_low = [(tile_ids >> i & 1).astype(jnp.float32) for i in range(10)]
    bits_row = [(group_ids >> i & 1).astype(jnp.float32) for i in range(spins - 10)]
    z_low = [1.0 - 2.0 * b for b in bits_low]
    z_row = [1.0 - 2.0 * b for b in bits_row]
    low_real = -sum(couplings[i] * z_low[i] * z_low[i + 1] for i in range(9))
    low_real = jnp.stack([low_real - couplings[9] * z_low[9], low_real + couplings[9] * z_low[9]])
    low_imag = -0.5 * sum(decays[i] * bits_low[i] for i in range(10))
    row_real = -sum(couplings[10 + i] * z_row[i] * z_row[i + 1] for i in range(spins - 11))
    row_imag = -0.5 * sum(decays[10 + i] * bits_row[i] for i in range(spins - 10))
    ids = jnp.arange(BLOCK, dtype=jnp.int32)
    crossed = ids[:, None] ^ ids[None, :]
    left = -sum(fields[7 + i] * (crossed == 1 << i).astype(jnp.float32) for i in range(8))
    right = -sum(
        fields[i if i < 7 else 15] * (crossed == 1 << i).astype(jnp.float32) for i in range(8)
    )

    def split(m):
        h = lax.reduce_precision(m, 8, 7)
        return [h.astype(jnp.bfloat16), (m - h).astype(jnp.bfloat16)]

    mats = jnp.stack(split(left) + split(right))
    smem = pl.BlockSpec(memory_space=pltpu.SMEM)
    vmem = pl.BlockSpec(memory_space=pltpu.VMEM)
    result = pl.pallas_call(
        functools.partial(kernel, spins, [start for start, _ in pieces]),
        out_shape=jax.ShapeDtypeStruct((2 * local_len // LANES, LANES), jnp.float32),
        in_specs=[smem] * 5 + [vmem] * (3 + len(pieces)),
        out_specs=vmem,
        scratch_shapes=[
            pltpu.VMEM((KRYLOV + 1, rows_total, LANES), jnp.float32),
            pltpu.VMEM((KRYLOV + 1, rows_total, LANES), jnp.float32),
            pltpu.VMEM((2, BLOCK, BLOCK), jnp.bfloat16),
            pltpu.VMEM((2, BLOCK, BLOCK), jnp.bfloat16),
            pltpu.VMEM((LANES, LANES), jnp.float32),
        ],
        compiler_params=pltpu.CompilerParams(vmem_limit_bytes=60 * 1024 * 1024),
        name="trajectory",
    )(
        fields,
        row_real,
        row_imag,
        channel.reshape(1),
        device.reshape(1).astype(jnp.int32),
        low_real,
        low_imag,
        mats,
        *[interleaved(piece) for _, piece in pieces],
    )
    rows = local_len // LANES
    return result.reshape(rows, 2, LANES).transpose(1, 0, 2).reshape(1, 2, local_len)


def solution(mesh):
    placed = (P("traj", None, "amp"), P(), P(), P(), P("traj"))
    return jax.shard_map(
        body, mesh=mesh, in_specs=placed, out_specs=P("traj", None, "amp"), check_vma=False
    )
```

time: 2200 us -> 164 us (0.07); the launches traced: 2170 us -> 162 us
  local copies, waits for them, and re-layouts: 1050 us -> 3.85 us
  other arithmetic: 535 us -> 36.3 us
  matrix products: 433 us -> 0 us
  blocking collectives: 110 us -> 0 us
  Pallas kernels: 0 us -> 107 us
  between operations: 25.7 us -> 0.74 us
    rev x19 -> x0, local copies, waits for them, and re-layouts: 514 us -> none  [flip_axis(): jnp.flip(tensor.reshape(new_shape), axis=axis_pos + 1).reshape(old_shape)]
    dot_general x61 -> x0, matrix products: 433 us -> none  [the longest x7 148 us: body(): jnp.einsum('tkcrl,tpcrl->tkp', stacked, paired, precision=highest)]
    reshape x43 -> x0, local copies, waits for them, and re-layouts: 317 us -> none  [the longest x19 180 us: flip_axis(): jnp.flip(tensor.reshape(new_shape), axis=axis_pos + 1).reshape(old_shape)]
    another operation x39 -> x0, local copies, waits for them, and re-layouts: 158 us -> none
    sub x86 -> x0, other arithmetic: 154 us -> none  [the longest x8 120 us: body(): out_imag = diag_real * imag_part + diag_imag * real_part - flipped[:, 1]]
    mul x81 -> x2, other arithmetic: 150 us -> 18 us  [the longest x1 11.2 us: body(): -0.5 * sum((decays[10 + i] * bits_row[i] for i in range(spins - 10)))]
    neg x9 -> x0, other arithmetic: 120 us -> none  [the longest x8 120 us: body(): swapped = jnp.stack([applied[:, 1], -applied[:, 0]], axis=1)]
    psum x10 -> x0, blocking collectives: 110 us -> none  [the longest x7 77.2 us: body(): projected, whole_sq = lax.psum((local_proj, local_sq), 'amp')]
  transfers between devices with their start and end apart: 18 -> 4, of which waited for: 1 -> 1; matrix products, arithmetic and copies ran while one was open for 21% -> 24% of each run, Pallas kernels for 0% -> 0%
where the time goes in v1:
time: 164 us; the launch traced here: 162 us
  Pallas kernels  107 us (65%)
  other arithmetic  36.3 us (22%)
  starting transfers between devices  7.85 us (5%)
  waiting for transfers between devices  5.92 us (4%)
  local copies, waits for them, and re-layouts  3.85 us (2%)
    pallas_call x1, Pallas kernels, body(): pl.pallas_call(functools.partial(kernel, spins, [start for start, _ in pi...  107 us
    mul x1, other arithmetic, body(): -0.5 * sum((decays[10 + i] * bits_row[i] for i in range(spins - 10)))  11.2 us
    convert_element_type x2, other arithmetic, split(): return [h.astype(jnp.bfloat16), (m - h).astype(jnp.bfloat16)]  10.4 us
    ppermute x4, starting transfers between devices, partner(): return lax.ppermute(value, 'amp', [(i, i ^ mask) for i in range(count)])  7.85 us
    mul x1, other arithmetic, body(): low_imag = -0.5 * sum((decays[i] * bits_low[i] for i in range(10)))  6.8 us
    add x1, other arithmetic, body(): low_real + couplings[9] * z_low[9]  6.45 us
    ppermute x4, waiting for transfers between devices, partner(): return lax.ppermute(value, 'amp', [(i, i ^ mask) for i in range(count)])  5.92 us
  transfers between devices with their start and end apart: 4, of which 1 were waited for; matrix products, arithmetic and copies ran while one was open for 24% of the time, Pallas kernels for 0%

profile of v1, /device:TPU:0, one launch (start us, length us, event | category | flops | bytes accessed | tf_op | source)
XLA Modules:
  0.0 161.7 jit_solution(17525300153048957784)
XLA Ops:
  0.0 3.0 %collective-permute-start.1 = (f32[1,2,131072]{2,1,0:T(2,128)}, f32[1,2,131072]{2,1,0:T(2,128)S(1)}, u32[]{:S(2)}, u32[]{:S(2)}) collective-permute-start(f32[1,2,131072]{2,1,0:T(2,128)} %param.5), channel_id=1, source_target_pairs={{0,2},{1,3},{2,0},{3,1},{4,6},{5,7},{6,4},{7,5},{8,10},{9,11},{10,... | collective-permute-start | bytes 3145736 | tf_op jit(solution)/shard_map/ppermute | solution.py:22
  3.0 1.5 collective-permute-start
  4.5 0.7 copy-done.4
  5.1 0.7 fusion.14
  5.9 0.0 copy-start.5
  5.9 6.8 %add_multiply_fusion.refs_6_ = f32[8,128]{1,0:T(8,128)} fusion(f32[]{:T(128)} %bitcast.37, f32[]{:T(128)} %bitcast.36, f32[]{:T(128)} %bitcast.35, f32[]{:T(128)} %bitcast.34, f32[]{:T(128)} %bitcast.33, f32[]{:T(128)} %bitcast.32, f32[]{:T(128)} %bitcast.31, f32[]{:T(128)} %bitcast.30, f32[]{:T(128)} %bitcast.29, f32[]{:T(128)} %bitcast.28), kind=kLoop, calls=%fused_computation.19 | loop fusion | flops 53248 | bytes 4136 | tf_op jit(solution)/shard_map/mul | solution.py:376
  12.7 0.0 copy-done.5
  12.7 0.7 fusion.15
  13.4 6.5 %fusion.11 = (f32[1,8,128]{2,1,0:T(8,128)S(1)}, f32[1,8,128]{2,1,0:T(8,128)S(1)}) fusion(f32[]{:T(128)} %bitcast.27, f32[]{:T(128)} %bitcast.26, f32[]{:T(128)} %bitcast.25, f32[]{:T(128)} %bitcast.24, f32[]{:T(128)} %bitcast.23, f32[]{:T(128)} %bitcast.22, f32[]{:T(128)} %bitcast.21, f32[]{:T(128)} %bitcast.20, f32[]{:T(128)} %bitcast.19, f32[]{:T(128)} %bitcast.18), kind=kLoop, calls=%fused_computation.24 | loop fusion | flops 83968 | bytes 8232 | tf_op jit(solution)/shard_map/add | solution.py:375
  19.9 0.6 pad_maximum_fusion.1.refs_5_
  20.4 5.9 %collective-permute-done.1 = f32[1,2,131072]{2,1,0:T(2,128)S(1)} collective-permute-done((f32[1,2,131072]{2,1,0:T(2,128)}, f32[1,2,131072]{2,1,0:T(2,128)S(1)}, u32[]{:S(2)}, u32[]{:S(2)}) %collective-permute-start.1) | collective-permute-done | bytes 1048608 | tf_op jit(solution)/shard_map/ppermute | solution.py:22
  26.4 1.8 %collective-permute-start.3 = (f32[1,2,65536]{2,1,0:T(2,128)S(1)}, f32[1,2,65536]{2,1,0:T(2,128)S(1)}, u32[]{:S(2)}, u32[]{:S(2)}) collective-permute-start(f32[1,2,65536]{2,1,0:T(2,128)S(1)} %slice.222), channel_id=1, source_target_pairs={{0,1},{1,0},{2,3},{3,2},{4,5},{5,4},{6,7},{7,6},{8,9},{9,8},{10,11... | collective-permute-start | bytes 1572872 | tf_op jit(solution)/shard_map/ppermute | solution.py:22
  28.2 0.0 collective-permute-done
  28.2 1.6 collective-permute-start.2
  29.8 11.2 %add_multiply_fusion.1 = (f32[512]{0:T(512)}, f32[512]{0:T(512)}) fusion(f32[]{:T(128)} %bitcast.16, f32[]{:T(128)} %bitcast.15, f32[]{:T(128)} %bitcast.14, f32[]{:T(128)} %bitcast.13, f32[]{:T(128)} %bitcast.12, f32[]{:T(128)} %bitcast.11, f32[]{:T(128)} %bitcast.10, f32[]{:T(128)} %bitcast.9, f32[]{:T(128)} %bitcast.8, s32[]{:T(128)S(6)} %mul.781, ...), kind=kLoop, calls=%fused_computation.26 | loop fusion | flops 45056 | bytes 4168 | tf_op jit(solution)/shard_map/mul | solution.py:378
  41.7 0.7 fusion.13
  42.4 5.2 %reduce-precision_convert_fusion.1 = (bf16[1,256,256]{2,1,0:T(8,128)(2,1)S(1)}, bf16[1,256,256]{2,1,0:T(8,128)(2,1)S(1)}) fusion(f32[]{:T(128)} %bitcast.45, f32[]{:T(128)} %bitcast.44, f32[]{:T(128)} %bitcast.43, f32[]{:T(128)} %bitcast.42, f32[]{:T(128)} %bitcast.41, f32[]{:T(128)} %bitcast.40, f32[]{:T(128)} %bitcast.39, f32[]{:T(128)} %bitcast.38), kind=kLoop, calls=%fused_computation.4 | loop fusion | flops 1900544 | bytes 262176 | tf_op jit(solution)/shard_map/convert_element_type | solution.py:388
  47.7 5.1 %reduce-precision_convert_fusion = (bf16[1,256,256]{2,1,0:T(8,128)(2,1)S(1)}, bf16[1,256,256]{2,1,0:T(8,128)(2,1)S(1)}) fusion(f32[]{:T(128)} %bitcast.53, f32[]{:T(128)} %bitcast.52, f32[]{:T(128)} %bitcast.51, f32[]{:T(128)} %bitcast.50, f32[]{:T(128)} %bitcast.49, f32[]{:T(128)} %bitcast.48, f32[]{:T(128)} %bitcast.47, f32[]{:T(128)} %bitcast.46), kind=kLoop, calls=%fused_computation.2 | loop fusion | flops 1900544 | bytes 262176 | tf_op jit(solution)/shard_map/convert_element_type | solution.py:388
  52.8 0.9 pad_maximum_fusion.refs_7_
  53.7 0.0 collective-permute-done.3
  53.7 0.0 collective-permute-done.2
  53.7 0.8 copy-done.2
  54.5 0.2 copy-done.3
  54.7 107.0 %trajectory.1 = f32[2048,128]{1,0:T(8,128)} custom-call(f32[19]{0:T(128)} %refs_0_.1, f32[512]{0:T(512)} %get-tuple-element.59.refs_1_, f32[512]{0:T(512)} %get-tuple-element.58.refs_2_, s32[1]{0:T(128)S(6)} %copy.12.refs_3_, s32[1]{0:T(128)} %bitcast.17.refs_4_, f32[2,8,128]{2,1,0:T(8,128)} %pad_maximum_fusion.1.refs_5_, ...), custom_call_target="tpu_custom_call" | custom-call | tf_op jit(solution)/shard_map/trajectory/pallas_call | solution.py:393
  (11 shorter events, 0.1 us)
Async XLA Ops:
  0.0 26.4 %collective-permute-start.1 = (f32[1,2,131072]{2,1,0:T(2,128)}, f32[1,2,131072]{2,1,0:T(2,128)S(1)}, u32[]{:S(2)}, u32[]{:S(2)}) collective-permute-start(f32[1,2,131072]{2,1,0:T(2,128)} %param.5), channel_id=1, source_target_pairs={{0,2},{1,3},{2,0},{3,1},{4,6},{5,7},{6,4},{7,5},{8,10},{9,11},{10,... | collective-permute-start | bytes 3145736 | tf_op jit(solution)/shard_map/ppermute | solution.py:22
  3.0 25.2 %collective-permute-start = (f32[1,2,131072]{2,1,0:T(2,128)}, f32[1,2,131072]{2,1,0:T(2,128)S(1)}, u32[]{:S(2)}, u32[]{:S(2)}) collective-permute-start(f32[1,2,131072]{2,1,0:T(2,128)} %param.5), channel_id=1, source_target_pairs={{0,1},{1,0},{2,3},{3,2},{4,5},{5,4},{6,7},{7,6},{8,9},{9,8},{10,11... | collective-permute-start | bytes 3145736 | tf_op jit(solution)/shard_map/ppermute | solution.py:22
  4.5 0.7 copy-start.4
  5.9 6.8 %copy-start.5 = (f32[18]{0:T(128)S(1)}, f32[18]{0:T(128)}, u32[]{:S(2)}) copy-start(f32[18]{0:T(128)} %param.6) | copy-start | bytes 220
  26.4 1.9 %copy-start = (f32[1,2,131072]{2,1,0:T(2,128)}, f32[1,2,131072]{2,1,0:T(2,128)S(1)}, u32[]{:S(2)}) copy-start(f32[1,2,131072]{2,1,0:T(2,128)S(1)} %collective-permute-done.1) | copy-start | bytes 3145732
  26.4 27.3 %collective-permute-start.3 = (f32[1,2,65536]{2,1,0:T(2,128)S(1)}, f32[1,2,65536]{2,1,0:T(2,128)S(1)}, u32[]{:S(2)}, u32[]{:S(2)}) collective-permute-start(f32[1,2,65536]{2,1,0:T(2,128)S(1)} %slice.222), channel_id=1, source_target_pairs={{0,1},{1,0},{2,3},{3,2},{4,5},{5,4},{6,7},{7,6},{8,9},{9,8},{10,11... | collective-permute-start | bytes 1572872 | tf_op jit(solution)/shard_map/ppermute | solution.py:22
  28.2 25.5 %copy-start.1 = (f32[1,2,131072]{2,1,0:T(2,128)}, f32[1,2,131072]{2,1,0:T(2,128)S(1)}, u32[]{:S(2)}) copy-start(f32[1,2,131072]{2,1,0:T(2,128)S(1)} %collective-permute-done) | copy-start | bytes 3145732
  28.2 25.5 %collective-permute-start.2 = (f32[1,2,65536]{2,1,0:T(2,128)S(1)}, f32[1,2,65536]{2,1,0:T(2,128)S(1)}, u32[]{:S(2)}, u32[]{:S(2)}) collective-permute-start(f32[1,2,65536]{2,1,0:T(2,128)S(1)} %slice.221), channel_id=1, source_target_pairs={{0,2},{1,3},{2,0},{3,1},{4,6},{5,7},{6,4},{7,5},{8,10},{9,11},{10,... | collective-permute-start | bytes 1572872 | tf_op jit(solution)/shard_map/ppermute | solution.py:22
  41.0 0.7 copy-start.6
  53.7 0.8 copy-start.2
  53.7 1.0 copy-start.3

commit v2 on v1

v2 whole, which is shorter than its diff:
```python
import functools
import jax
import jax.numpy as jnp
from jax import lax
from jax.experimental import pallas as pl
from jax.experimental.pallas import tpu as pltpu
from jax.sharding import PartitionSpec as P

KRYLOV = 8
time_step = 0.7
squarings = 8
taylor_order = 10
highest = lax.Precision.HIGHEST
LANES = 128
TILE = (8, LANES)
BLOCK = 256
CHUNK = 2 * BLOCK
SET_BITS = 2


def partner(value, mask):
    count = lax.axis_size("amp")
    return lax.ppermute(value, "amp", [(i, i ^ mask) for i in range(count)])


def gather_state(own, high_bits):
    rows = own.shape[2] // LANES
    if high_bits == 2:
        half = own.shape[2] // 2
        first = partner(own, 1)
        second = partner(own, 2)
        third_low = partner(first[:, :, :half], 2)
        third_high = partner(second[:, :, half:], 1)
        return [
            (0, own),
            (rows, first),
            (2 * rows, second),
            (3 * rows, third_low),
            (3 * rows + rows // 2, third_high),
        ]
    pieces = [(0, own)]
    for bit in range(high_bits):
        pieces += [(start + (rows << bit), partner(piece, 1 << bit)) for start, piece in pieces]
    return pieces


def interleaved(piece):
    rows = piece.shape[2] // LANES
    return piece.reshape(2, rows, LANES).transpose(1, 0, 2).reshape(2 * rows, LANES)


def splat(value):
    return jnp.broadcast_to(value, TILE)


def total(acc):
    return splat(jnp.sum(acc, keepdims=True))


def cmul(a, b):
    return (a[0] * b[0] - a[1] * b[1], a[0] * b[1] + a[1] * b[0])


def conj(a):
    return (a[0], -a[1])


def sub(a, b):
    return (a[0] - b[0], a[1] - b[1])


def scale(a, r):
    return (a[0] * r, a[1] * r)


def prepare(spins, couplings, fields, decays, device, mats, low, rows):
    tile_ids = lax.broadcasted_iota(jnp.int32, TILE, 0) * LANES + lax.broadcasted_iota(jnp.int32, TILE, 1)
    bits = [(tile_ids >> i & 1).astype(jnp.float32) for i in range(10)]
    signs = [1.0 - 2.0 * b for b in bits]
    real = -sum(couplings[i] * (signs[i] * signs[i + 1]) for i in range(9))
    bond = couplings[9] * signs[9]
    low[0:8, :] = real - bond
    low[8:16, :] = real + bond
    low[16:24, :] = -0.5 * sum(decays[i] * bits[i] for i in range(10))
    low[24:32, :] = jnp.zeros(TILE, jnp.float32)
    wide = rows.shape
    ids = lax.broadcasted_iota(jnp.int32, wide, 1) ^ device[0]
    bits = [(ids >> i & 1).astype(jnp.float32) for i in range(spins - 10)]
    signs = [1.0 - 2.0 * b for b in bits]
    real = -sum(couplings[10 + i] * (signs[i] * signs[i + 1]) for i in range(spins - 11))
    imag = -0.5 * sum(decays[10 + i] * bits[i] for i in range(spins - 10))
    rows[...] = jnp.where(lax.broadcasted_iota(jnp.int32, wide, 0) == 0, real, imag)
    for r in range(0, BLOCK, 32):
        shape = (32, BLOCK)
        crossed = (r + lax.broadcasted_iota(jnp.int32, shape, 0)) ^ lax.broadcasted_iota(jnp.int32, shape, 1)
        for side in range(2):
            m = jnp.zeros(shape, jnp.float32)
            for i in range(8):
                spin = 7 + i if side == 0 else (i if i < 7 else 15)
                m = jnp.where(crossed == 1 << i, -fields[spin], m)
            h = m.astype(jnp.bfloat16)
            mats[2 * side, r : r + 32, :] = h
            mats[2 * side + 1, r : r + 32, :] = (m - h.astype(jnp.float32)).astype(jnp.bfloat16)


def kernel(spins, starts, *refs):
    count = len(starts)
    fields, row_table, channel, device = refs[:4]
    low_table, mats = refs[4:6]
    pieces = refs[6 : 6 + count]
    out = refs[6 + count]
    basis_r, basis_i, cur_r, cur_i, new_r, new_i, high, low, table, coefs, norms, inner_r, inner_i = refs[7 + count :]
    rows_total = new_r.shape[0]
    groups = rows_total // 8
    rows_out = out.shape[0] // 2
    zero = jnp.zeros(TILE, jnp.float32)
    dot = functools.partial(jnp.dot, preferred_element_type=jnp.float32)

    for start, piece in zip(starts, pieces):

        def take(g, carry, start=start, piece=piece):
            row = pl.multiple_of(start + g * 8, 8)
            new_r[pl.ds(row, 8), :] = piece[pl.ds(pl.multiple_of(g * 16, 16), 8, stride=2), :]
            new_i[pl.ds(row, 8), :] = piece[pl.ds(g * 16 + 1, 8, stride=2), :]
            return carry

        lax.fori_loop(0, piece.shape[0] // 16, take, 0, unroll=8)

    def block_flips(c):
        base = pl.multiple_of(c * CHUNK, CHUNK)
        for part, ref in ((0, new_r), (1, new_i)):
            xh, xl = high[part, c], low[part, c]
            y = dot(mats[0], xh) + dot(mats[1], xh) + dot(mats[0], xl)
            y = y + dot(xh, mats[2]) + dot(xh, mats[3]) + dot(xl, mats[2])
            ref[pl.ds(base, BLOCK), :] = y[:, :LANES]
            ref[pl.ds(base + BLOCK, BLOCK), :] = y[:, LANES:]

    def halves(part, c, block, r, value):
        h = value.astype(jnp.bfloat16)
        l = (value - h.astype(jnp.float32)).astype(jnp.bfloat16)
        high[part, c, pl.ds(r, 16), pl.ds(block * LANES, LANES)] = h
        low[part, c, pl.ds(r, 16), pl.ds(block * LANES, LANES)] = l

    near = [(b, fields[7 + b]) for b in range(9, 9 + SET_BITS)]
    far = [(b, fields[7 + b]) for b in range(9 + SET_BITS, spins - 7)]
    sets = 1 << SET_BITS
    span = CHUNK * sets
    ones = jnp.ones(TILE, jnp.float32)
    for i, value in enumerate((ones, zero, zero, zero)):
        coefs[i] = value

    def clear(t, carry):
        at = pl.ds(pl.multiple_of(t * 8, 8), 8)
        for ref in (cur_r, cur_i, basis_r.at[0], basis_i.at[0]):
            ref[at, :] = zero
        return carry

    lax.fori_loop(0, groups, clear, 0, unroll=8)

    def one_step(step):
        earlier = jnp.maximum(step - 2, 0)

        def make(t, acc):
            start = pl.multiple_of(t * span, span)
            sc, ar, ai, b = [jnp.concatenate([coefs[i], coefs[i]]) for i in range(4)]
            lr, li = (low_table[0:8, :], low_table[8:16, :]), low_table[16:24, :]

            def vector(i, acc):
                for block in range(2):
                    for r in range(0, BLOCK, 16):
                        at = pl.ds(start + i * CHUNK + block * BLOCK + r, 16)
                        pr, pi = cur_r[at, :], cur_i[at, :]
                        re = sc * new_r[at, :] - (ar * pr - ai * pi) - b * basis_r[earlier, at, :]
                        im = sc * new_i[at, :] - (ar * pi + ai * pr) - b * basis_i[earlier, at, :]
                        cur_r[at, :] = re
                        cur_i[at, :] = im
                        sq = re * re + im * im
                        acc = acc + (sq[:8] + sq[8:])
                        c = t * sets + i
                        halves(0, c, block, r, re)
                        halves(1, c, block, r, im)
                return acc

            def rest(i):
                for r in range(0, CHUNK, 8):
                    row = i * CHUNK + r
                    at = pl.ds(start + row, 8)
                    xr, xi = cur_r[at, :], cur_i[at, :]
                    wr, wi = new_r[at, :], new_i[at, :]
                    g = t * (span // 8) + row // 8
                    dr = lr[(r // 8) & 1] + row_table[0, g]
                    di = li + row_table[1, g]
                    wr = wr + (dr * xr - di * xi)
                    wi = wi + (dr * xi + di * xr)
                    for bit, weight in near:
                        other = pl.ds(start + (row ^ (1 << bit)), 8)
                        wr = wr - weight * cur_r[other, :]
                        wi = wi - weight * cur_i[other, :]
                    new_r[at, :] = wr
                    new_i[at, :] = wi

            for i in range(sets):
                acc = vector(i, acc)
                block_flips(t * sets + i)
            for i in range(sets):
                rest(i)
            return acc

        norms[step] = total(lax.fori_loop(0, rows_total // span, make, zero))

    def products(step):
        count_rows = 32 if step < 2 else 16 if step < 5 else 8

        def apply(t, accs):
            base = pl.multiple_of(t * (8 * count_rows), 8 * count_rows)
            at = [pl.ds(pl.multiple_of(base + 8 * r, 8), 8) for r in range(count_rows)]
            w = []
            for r in range(count_rows):
                wr, wi = new_r[at[r], :], new_i[at[r], :]
                for bit, weight in far:
                    other = pl.ds(pl.multiple_of((base ^ (1 << bit)) + 8 * r, 8), 8)
                    wr = wr - weight * cur_r[other, :]
                    wi = wi - weight * cur_i[other, :]
                if step + 1 < KRYLOV:
                    new_r[at[r], :] = wr
                    new_i[at[r], :] = wi
                w.append((wr, wi))
            accs = list(accs)
            for k in range(step + 1):
                re, im = [], []
                for r in range(count_rows):
                    if k == step:
                        ur, ui = cur_r[at[r], :], cur_i[at[r], :]
                        basis_r[k, at[r], :] = ur
                        basis_i[k, at[r], :] = ui
                    else:
                        ur, ui = basis_r[k, at[r], :], basis_i[k, at[r], :]
                    wr, wi = w[r]
                    re.append(ur * wr + ui * wi)
                    im.append(ur * wi - ui * wr)
                    if len(re) == 4:
                        accs[2 * k] = accs[2 * k] + ((re[0] + re[1]) + (re[2] + re[3]))
                        accs[2 * k + 1] = accs[2 * k + 1] + ((im[0] + im[1]) + (im[2] + im[3]))
                        re, im = [], []
            return tuple(accs)

        sums = lax.fori_loop(0, groups // count_rows, apply, (zero,) * (2 * step + 2))
        unit = lax.rsqrt(norms[0]) if step == 0 else ones
        found = [total(x) * unit for x in sums]
        for k in range(step + 1):
            inner_r[step * KRYLOV + k] = found[2 * k]
            inner_i[step * KRYLOV + k] = found[2 * k + 1]
        inverse = 1.0 / norms[step]
        coefs[0] = unit
        coefs[1] = found[2 * step] * inverse
        coefs[2] = found[2 * step + 1] * inverse
        coefs[3] = found[2 * step - 2] / norms[step - 1] if step > 0 else zero

    @pl.loop(0, KRYLOV)
    def _(step):
        one_step(step)
        for s in range(KRYLOV):
            pl.when(step == s)(functools.partial(products, s))

    norm = [norms[j] for j in range(KRYLOV)]
    gram, diag_a, real_b = {(0, 0): (norm[0], zero)}, [], []
    read = lambda k, j: (inner_r[j * KRYLOV + k], inner_i[j * KRYLOV + k])
    g = lambda i, j: gram[i, j] if i <= j else conj(gram[j, i])
    for j in range(KRYLOV - 1):
        diag_a.append(scale(read(j, j), 1.0 / norm[j]))
        real_b.append(read(j - 1, j)[0] / norm[j - 1] if j > 0 else zero)
        for k in range(j + 1):
            value = sub(read(k, j), cmul(diag_a[j], g(k, j)))
            if j > 0:
                value = sub(value, scale(g(k, j - 1), real_b[j]))
            gram[k, j + 1] = value
        gram[j + 1, j + 1] = (norm[j + 1], zero)
    inner = [read(k, KRYLOV - 1) for k in range(KRYLOV)]

    size = [jnp.sqrt(x) for x in norm]
    inv = [1.0 / x for x in size]
    mat = {}
    for j in range(KRYLOV):
        for k in range(j + 1):
            mat[j, k] = conj(scale(gram[k, j], inv[k] * inv[j]))
    rhs = [scale(inner[k], inv[k] * inv[KRYLOV - 1]) for k in range(KRYLOV)]
    factor, pivot = {}, []
    for j in range(KRYLOV):
        d = mat[j, j][0]
        for k in range(j):
            d = d - (factor[j, k][0] * factor[j, k][0] + factor[j, k][1] * factor[j, k][1]) * pivot[k]
        pivot.append(d)
        r = 1.0 / d
        for i in range(j + 1, KRYLOV):
            x = mat[i, j]
            for k in range(j):
                x = sub(x, scale(cmul(factor[i, k], conj(factor[j, k])), pivot[k]))
            factor[i, j] = scale(x, r)
    last = list(rhs)
    for i in range(KRYLOV):
        for k in range(i):
            last[i] = sub(last[i], cmul(factor[i, k], last[k]))
    last = [scale(x, 1.0 / pivot[i]) for i, x in enumerate(last)]
    for i in reversed(range(KRYLOV)):
        for k in range(i + 1, KRYLOV):
            last[i] = sub(last[i], cmul(conj(factor[k, i]), last[k]))

    entries = {}
    for j in range(KRYLOV - 1):
        entries[j, j] = diag_a[j] if j > 0 else scale(diag_a[0], size[0])
        grow = size[1] if j == 0 else size[j + 1] * inv[j]
        entries[j + 1, j] = (grow, zero)
        if j > 0:
            entries[j - 1, j] = (real_b[j] * (size[j - 1] * inv[j]), zero)
    for i in range(KRYLOV):
        entries[i, KRYLOV - 1] = last[i]
    order = 2 * KRYLOV
    code = lax.broadcasted_iota(jnp.int32, TILE, 0) * LANES + lax.broadcasted_iota(jnp.int32, TILE, 1)
    quads = [[zero, zero], [zero, zero]]
    for (i, j), (re, im) in entries.items():
        here = code == i * LANES + j
        there = code == i * LANES + j + KRYLOV
        ar, ai = time_step * im, -time_step * re
        quads[0][0] = jnp.where(here, ar, jnp.where(there, -ai, quads[0][0]))
        quads[1][0] = jnp.where(here, ai, jnp.where(there, ar, quads[1][0]))
    table[...] = jnp.zeros_like(table)
    table[0:8, :] = quads[0][0] * (1.0 / 2.0**squarings)
    table[8:16, :] = quads[1][0] * (1.0 / 2.0**squarings)
    one = table[0:order, :]
    eye = jnp.where(
        lax.broadcasted_iota(jnp.int32, one.shape, 0) == lax.broadcasted_iota(jnp.int32, one.shape, 1), 1.0, 0.0
    )
    fill = jnp.zeros((LANES - order, LANES), jnp.float32)

    def times(a, b):
        return dot(a, jnp.concatenate([b, fill]), precision=highest)

    two = times(one, one)
    three = times(two, one)
    f = [1.0]
    for d in range(1, taylor_order + 1):
        f.append(f[-1] / d)
    series = f[9] * eye + f[10] * one
    for d in (6, 3, 0):
        series = (f[d] * eye + f[d + 1] * one + f[d + 2] * two) + times(three, series)
    for repeat in range(squarings):
        series = times(series, series)
    table[0:order, :] = series
    weights = []
    for k in range(KRYLOV):
        c = size[0] * inv[k]
        weights.append((splat(table[k : k + 1, 0:1]) * c, splat(table[k + 8 : k + 9, 0:1]) * c))

    jump = channel[0]
    first = device[0]
    lane = lax.broadcasted_iota(jnp.int32, TILE, 1)
    sublane = lax.broadcasted_iota(jnp.int32, TILE, 0)
    inside = sublane * LANES + lane
    far_jump = jump >= 10
    low_bit = jnp.where(far_jump, 0, jump)
    high_bit = jnp.where(far_jump, jump - 10, 0)
    set_low = ((inside >> low_bit) & 1) == 1
    groups_out = rows_out // 8
    absolute = first * groups_out

    def combine(c, acc):
        for r in range(4):
            g = c * 4 + r
            at = pl.ds(pl.multiple_of(g * 8, 8), 8)
            pr, pi = zero, zero
            for k in range(KRYLOV):
                cr, ci = weights[k]
                ur, ui = basis_r[k, at, :], basis_i[k, at, :]
                pr = pr + (cr * ur - ci * ui)
                pi = pi + (cr * ui + ci * ur)
            new_r[at, :] = pr
            new_i[at, :] = pi
            raised = jnp.where(far_jump, ((g ^ absolute) >> high_bit) & 1, 1)
            acc = acc + raised.astype(jnp.float32) * (pr * pr + pi * pi)
        return acc

    weight = lax.fori_loop(0, groups // 4, combine, zero)
    weight = total(jnp.where(set_low | far_jump, weight, 0.0))
    gain = jnp.sqrt((rows_total * LANES) / weight)

    def put(g, re, im):
        out[pl.ds(pl.multiple_of(g * 16, 16), 8, stride=2), :] = re
        out[pl.ds(g * 16 + 1, 8, stride=2), :] = im

    def stay(g, _):
        at = pl.ds(pl.multiple_of(g * 8, 8), 8)
        put(g, new_r[at, :], new_i[at, :])
        return 0

    def lower_far(g, _):
        at = pl.ds(pl.multiple_of((g ^ (1 << high_bit)) * 8, 8), 8)
        vacant = 1 - (((g ^ absolute) >> high_bit) & 1)
        factor = gain * vacant.astype(jnp.float32)
        put(g, factor * new_r[at, :], factor * new_i[at, :])
        return 0

    def lower_lane(g, _):
        at = pl.ds(pl.multiple_of(g * 8, 8), 8)
        shift = LANES - (1 << low_bit)
        factor = jnp.where(set_low, 0.0, gain)
        put(
            g,
            factor * pltpu.roll(new_r[at, :], shift, 1),
            factor * pltpu.roll(new_i[at, :], shift, 1),
        )
        return 0

    def lower_sublane(bit):
        def run(g, _):
            at = pl.ds(pl.multiple_of(g * 8, 8), 8)
            shift = 8 - (1 << bit)
            factor = jnp.where(set_low, 0.0, gain)
            put(
                g,
                factor * pltpu.roll(new_r[at, :], shift, 0),
                factor * pltpu.roll(new_i[at, :], shift, 0),
            )
            return 0

        return run

    def over_output(run):
        lax.fori_loop(0, groups_out, run, 0, unroll=4)

    pl.when(jump == spins)(lambda: over_output(stay))
    pl.when((jump >= 10) & (jump < spins))(lambda: over_output(lower_far))
    pl.when(jump < 7)(lambda: over_output(lower_lane))
    for bit in range(3):
        pl.when(jump == 7 + bit)(functools.partial(over_output, lower_sublane(bit)))


def body(amplitudes, couplings, fields, decays, channel):
    node_count = lax.axis_size("amp")
    high_bits = node_count.bit_length() - 1
    device = lax.axis_index("amp")
    local_len = amplitudes.shape[2]
    spins = fields.shape[0]
    rows_total = node_count * local_len // LANES
    groups = rows_total // 8
    pieces = gather_state(amplitudes, high_bits)

    smem = pl.BlockSpec(memory_space=pltpu.SMEM)
    vmem = pl.BlockSpec(memory_space=pltpu.VMEM)
    mats, low, row_table = pl.pallas_call(
        functools.partial(prepare, spins),
        out_shape=(
            jax.ShapeDtypeStruct((4, BLOCK, BLOCK), jnp.bfloat16),
            jax.ShapeDtypeStruct((32, LANES), jnp.float32),
            jax.ShapeDtypeStruct((8, groups), jnp.float32),
        ),
        in_specs=[smem] * 4,
        out_specs=(vmem, vmem, vmem),
        cost_estimate=pl.CostEstimate(flops=20_000_000, bytes_accessed=1_000_000, transcendentals=0),
        name="tables",
    )(couplings, fields, decays, (device * (local_len // LANES // 8)).reshape(1).astype(jnp.int32))
    result = pl.pallas_call(
        functools.partial(kernel, spins, [start for start, _ in pieces]),
        out_shape=jax.ShapeDtypeStruct((2 * local_len // LANES, LANES), jnp.float32),
        in_specs=[smem] * 4 + [vmem] * (2 + len(pieces)),
        out_specs=vmem,
        scratch_shapes=[
            pltpu.VMEM((KRYLOV, rows_total, LANES), jnp.float32),
            pltpu.VMEM((KRYLOV, rows_total, LANES), jnp.float32),
            pltpu.VMEM((rows_total, LANES), jnp.float32),
            pltpu.VMEM((rows_total, LANES), jnp.float32),
            pltpu.VMEM((rows_total, LANES), jnp.float32),
            pltpu.VMEM((rows_total, LANES), jnp.float32),
            pltpu.VMEM((2, rows_total // CHUNK, BLOCK, BLOCK), jnp.bfloat16),
            pltpu.VMEM((2, rows_total // CHUNK, BLOCK, BLOCK), jnp.bfloat16),
            pltpu.VMEM((LANES, LANES), jnp.float32),
            pltpu.VMEM((4,) + TILE, jnp.float32),
            pltpu.VMEM((KRYLOV,) + TILE, jnp.float32),
            pltpu.VMEM((KRYLOV * KRYLOV,) + TILE, jnp.float32),
            pltpu.VMEM((KRYLOV * KRYLOV,) + TILE, jnp.float32),
        ],
        compiler_params=pltpu.CompilerParams(vmem_limit_bytes=60 * 1024 * 1024),
        name="trajectory",
    )(
        fields,
        row_table,
        channel.reshape(1),
        device.reshape(1).astype(jnp.int32),
        low,
        mats,
        *[interleaved(piece) for _, piece in pieces],
    )
    rows = local_len // LANES
    return result.reshape(rows, 2, LANES).transpose(1, 0, 2).reshape(1, 2, local_len)


def solution(mesh):
    placed = (P("traj", None, "amp"), P(), P(), P(), P("traj"))
    return jax.shard_map(
        body, mesh=mesh, in_specs=placed, out_specs=P("traj", None, "amp"), check_vma=False
    )
```

time: 164 us -> 133 us (0.81); the launches traced: 162 us -> 133 us
  other arithmetic: 36.3 us -> 0 us
  waiting for transfers between devices: 5.92 us -> 30.7 us
  Pallas kernels: 107 us -> 91 us
    ppermute x4, waiting for transfers between devices: 5.92 us -> 30.7 us  [partner(): return lax.ppermute(value, 'amp', [(i, i ^ mask) for i in range(count)])]
    mul x2 -> x0, other arithmetic: 18 us -> none  [the longest x1 11.2 us: body(): -0.5 * sum((decays[10 + i] * bits_row[i] for i in range(spins - 10)))]
    pallas_call x1, Pallas kernels: 107 us -> 89.3 us  [body(): pl.pallas_call(functools.partial(kernel, spins, [start for start, _ in pi...]
    convert_element_type x2 -> x0, other arithmetic: 10.4 us -> none  [split(): return [h.astype(jnp.bfloat16), (m - h).astype(jnp.bfloat16)]]
    add x1 -> x0, other arithmetic: 6.45 us -> none  [body(): low_real + couplings[9] * z_low[9]]
    slice x3 -> x0, local copies, waits for them, and re-layouts: 2.16 us -> none  [the longest x1 0.72 us: body(): low_imag = -0.5 * sum((decays[i] * bits_low[i] for i in range(10)))]
    pallas_call x0 -> x1, Pallas kernels: none -> 1.76 us  [body(): pl.pallas_call(functools.partial(prepare, spins), out_shape=(jax.ShapeDty...]
  transfers between devices with their start and end apart: 4 -> 4, of which waited for: 1 -> 3; matrix products, arithmetic and copies ran while one was open for 24% -> 1% of each run, Pallas kernels for 0% -> 1%
where the time goes in v2:
time: 133 us
  Pallas kernels  91 us (68%)
  waiting for transfers between devices  30.7 us (23%)
  starting transfers between devices  7.72 us (6%)
  local copies, waits for them, and re-layouts  2.59 us (2%)
    pallas_call x1, Pallas kernels, body(): pl.pallas_call(functools.partial(kernel, spins, [start for start, _ in pi...  89.3 us
    ppermute x4, waiting for transfers between devices, partner(): return lax.ppermute(value, 'amp', [(i, i ^ mask) for i in range(count)])  30.7 us
    ppermute x4, starting transfers between devices, partner(): return lax.ppermute(value, 'amp', [(i, i ^ mask) for i in range(count)])  7.72 us
  transfers between devices with their start and end apart: 4, of which 3 were waited for; matrix products, arithmetic and copies ran while one was open for 1% of the time, Pallas kernels for 1%

profile of v2, /device:TPU:0, one launch (start us, length us, event | category | flops | bytes accessed | tf_op | source)
XLA Modules:
  0.0 132.7 jit_solution(8509410932822033874)
XLA Ops:
  0.0 3.0 %collective-permute-start.1 = (f32[1,2,131072]{2,1,0:T(2,128)}, f32[1,2,131072]{2,1,0:T(2,128)S(1)}, u32[]{:S(2)}, u32[]{:S(2)}) collective-permute-start(f32[1,2,131072]{2,1,0:T(2,128)} %param.5), channel_id=1, source_target_pairs={{0,2},{1,3},{2,0},{3,1},{4,6},{5,7},{6,4},{7,5},{8,10},{9,11},{10,... | collective-permute-start | bytes 3145736 | tf_op jit(solution)/shard_map/ppermute | solution.py:23
  3.0 1.5 %collective-permute-start = (f32[1,2,131072]{2,1,0:T(2,128)}, f32[1,2,131072]{2,1,0:T(2,128)S(1)}, u32[]{:S(2)}, u32[]{:S(2)}) collective-permute-start(f32[1,2,131072]{2,1,0:T(2,128)} %param.5), channel_id=1, source_target_pairs={{0,1},{1,0},{2,3},{3,2},{4,5},{5,4},{6,7},{7,6},{8,9},{9,8},{10,11... | collective-permute-start | bytes 3145736 | tf_op jit(solution)/shard_map/ppermute | solution.py:23
  4.5 21.9 %collective-permute-done.1 = f32[1,2,131072]{2,1,0:T(2,128)S(1)} collective-permute-done((f32[1,2,131072]{2,1,0:T(2,128)}, f32[1,2,131072]{2,1,0:T(2,128)S(1)}, u32[]{:S(2)}, u32[]{:S(2)}) %collective-permute-start.1) | collective-permute-done | bytes 1048608 | tf_op jit(solution)/shard_map/ppermute | solution.py:23
  26.4 0.0 copy-start
  26.4 0.9 slice.9
  27.3 1.7 %collective-permute-start.3 = (f32[1,2,65536]{2,1,0:T(2,128)}, f32[1,2,65536]{2,1,0:T(2,128)S(1)}, u32[]{:S(2)}, u32[]{:S(2)}) collective-permute-start(f32[1,2,65536]{2,1,0:T(2,128)} %slice.9), channel_id=1, source_target_pairs={{0,1},{1,0},{2,3},{3,2},{4,5},{5,4},{6,7},{7,6},{8,9},{9,8},{10,11... | collective-permute-start | bytes 1572872 | tf_op jit(solution)/shard_map/ppermute | solution.py:23
  29.0 0.0 collective-permute-done
  29.0 0.0 copy-start.1
  29.0 0.9 slice.8
  29.9 0.0 copy-done
  29.9 1.5 %collective-permute-start.2 = (f32[1,2,65536]{2,1,0:T(2,128)}, f32[1,2,65536]{2,1,0:T(2,128)S(1)}, u32[]{:S(2)}, u32[]{:S(2)}) collective-permute-start(f32[1,2,65536]{2,1,0:T(2,128)} %slice.8), channel_id=1, source_target_pairs={{0,2},{1,3},{2,0},{3,1},{4,6},{5,7},{6,4},{7,5},{8,10},{9,11},{10,... | collective-permute-start | bytes 1572872 | tf_op jit(solution)/shard_map/ppermute | solution.py:23
  32.0 1.8 %tables.1 = (bf16[4,256,256]{2,1,0:T(8,128)(2,1)}, f32[32,128]{1,0:T(8,128)}, f32[8,512]{1,0:T(8,128)}) custom-call(f32[18]{0:T(128)} %couplings.1, f32[19]{0:T(128)} %refs_0_.1, f32[19]{0:T(128)} %decays.1, s32[1]{0:T(128)} %bitcast.device), custom_call_target="tpu_custom_call" | custom-call | flops 20000000 | bytes 1000000 | tf_op jit(solution)/shard_map/tables/pallas_call | solution.py:449
  33.8 6.8 %collective-permute-done.3 = f32[1,2,65536]{2,1,0:T(2,128)S(1)} collective-permute-done((f32[1,2,65536]{2,1,0:T(2,128)}, f32[1,2,65536]{2,1,0:T(2,128)S(1)}, u32[]{:S(2)}, u32[]{:S(2)}) %collective-permute-start.3) | collective-permute-done | bytes 524320 | tf_op jit(solution)/shard_map/ppermute | solution.py:23
  40.6 0.0 copy-start.2
  40.6 2.0 %collective-permute-done.2 = f32[1,2,65536]{2,1,0:T(2,128)S(1)} collective-permute-done((f32[1,2,65536]{2,1,0:T(2,128)}, f32[1,2,65536]{2,1,0:T(2,128)S(1)}, u32[]{:S(2)}, u32[]{:S(2)}) %collective-permute-start.2) | collective-permute-done | bytes 524320 | tf_op jit(solution)/shard_map/ppermute | solution.py:23
  42.6 0.0 copy-start.3
  42.6 0.0 copy-done.1
  42.6 0.0 copy-done.2
  42.6 0.8 copy-done.3
  43.4 89.3 %trajectory.1 = f32[2048,128]{1,0:T(8,128)} custom-call(f32[19]{0:T(128)} %refs_0_.1, f32[8,512]{1,0:T(8,128)} %get-tuple-element.8.refs_1_, s32[1]{0:T(128)S(6)} %copy.12.refs_2_, s32[1]{0:T(128)} %bitcast.1.refs_3_, f32[32,128]{1,0:T(8,128)} %get-tuple-element.9.refs_4_, bf16[4,256,256]{2,1,0:T(8,128)(2,1)} %get-tuple-element.10.refs_5_, ...), custom_call_target="tpu_custom_call" | custom-call | tf_op jit(solution)/shard_map/trajectory/pallas_call | solution.py:461
Async XLA Ops:
  0.0 26.4 %collective-permute-start.1 = (f32[1,2,131072]{2,1,0:T(2,128)}, f32[1,2,131072]{2,1,0:T(2,128)S(1)}, u32[]{:S(2)}, u32[]{:S(2)}) collective-permute-start(f32[1,2,131072]{2,1,0:T(2,128)} %param.5), channel_id=1, source_target_pairs={{0,2},{1,3},{2,0},{3,1},{4,6},{5,7},{6,4},{7,5},{8,10},{9,11},{10,... | collective-permute-start | bytes 3145736 | tf_op jit(solution)/shard_map/ppermute | solution.py:23
  3.0 26.0 %collective-permute-start = (f32[1,2,131072]{2,1,0:T(2,128)}, f32[1,2,131072]{2,1,0:T(2,128)S(1)}, u32[]{:S(2)}, u32[]{:S(2)}) collective-permute-start(f32[1,2,131072]{2,1,0:T(2,128)} %param.5), channel_id=1, source_target_pairs={{0,1},{1,0},{2,3},{3,2},{4,5},{5,4},{6,7},{7,6},{8,9},{9,8},{10,11... | collective-permute-start | bytes 3145736 | tf_op jit(solution)/shard_map/ppermute | solution.py:23
  26.4 3.5 %copy-start = (f32[1,2,131072]{2,1,0:T(2,128)}, f32[1,2,131072]{2,1,0:T(2,128)S(1)}, u32[]{:S(2)}) copy-start(f32[1,2,131072]{2,1,0:T(2,128)S(1)} %collective-permute-done.1) | copy-start | bytes 3145732
  27.3 13.3 %collective-permute-start.3 = (f32[1,2,65536]{2,1,0:T(2,128)}, f32[1,2,65536]{2,1,0:T(2,128)S(1)}, u32[]{:S(2)}, u32[]{:S(2)}) collective-permute-start(f32[1,2,65536]{2,1,0:T(2,128)} %slice.9), channel_id=1, source_target_pairs={{0,1},{1,0},{2,3},{3,2},{4,5},{5,4},{6,7},{7,6},{8,9},{9,8},{10,11... | collective-permute-start | bytes 1572872 | tf_op jit(solution)/shard_map/ppermute | solution.py:23
  29.0 13.6 %copy-start.1 = (f32[1,2,131072]{2,1,0:T(2,128)}, f32[1,2,131072]{2,1,0:T(2,128)S(1)}, u32[]{:S(2)}) copy-start(f32[1,2,131072]{2,1,0:T(2,128)S(1)} %collective-permute-done) | copy-start | bytes 3145732
  29.9 12.7 %collective-permute-start.2 = (f32[1,2,65536]{2,1,0:T(2,128)}, f32[1,2,65536]{2,1,0:T(2,128)S(1)}, u32[]{:S(2)}, u32[]{:S(2)}) collective-permute-start(f32[1,2,65536]{2,1,0:T(2,128)} %slice.8), channel_id=1, source_target_pairs={{0,2},{1,3},{2,0},{3,1},{4,6},{5,7},{6,4},{7,5},{8,10},{9,11},{10,... | collective-permute-start | bytes 1572872 | tf_op jit(solution)/shard_map/ppermute | solution.py:23
  40.6 2.1 %copy-start.2 = (f32[1,2,65536]{2,1,0:T(2,128)}, f32[1,2,65536]{2,1,0:T(2,128)S(1)}, u32[]{:S(2)}) copy-start(f32[1,2,65536]{2,1,0:T(2,128)S(1)} %collective-permute-done.3) | copy-start | bytes 1572868
  42.6 0.8 copy-start.3

commit v3 on v2

--- a/solution.py
+++ b/solution.py
@@ -27,17 +27,13 @@
     rows = own.shape[2] // LANES
     if high_bits == 2:
         half = own.shape[2] // 2
-        first = partner(own, 1)
-        second = partner(own, 2)
-        third_low = partner(first[:, :, :half], 2)
-        third_high = partner(second[:, :, half:], 1)
-        return [
-            (0, own),
-            (rows, first),
-            (2 * rows, second),
-            (3 * rows, third_low),
-            (3 * rows + rows // 2, third_high),
-        ]
+        low, high = own[:, :, :half], own[:, :, half:]
+        first_low, second_high = partner(low, 1), partner(high, 2)
+        first_high, second_low = partner(high, 1), partner(low, 2)
+        third_low, third_high = partner(first_low, 2), partner(second_high, 1)
+        parts = [own, first_low, first_high, second_low, second_high, third_low, third_high]
+        starts = [0, rows, rows + rows // 2, 2 * rows, 2 * rows + rows // 2, 3 * rows, 3 * rows + rows // 2]
+        return list(zip(starts, parts))
     pieces = [(0, own)]
     for bit in range(high_bits):
         pieces += [(start + (rows << bit), partner(piece, 1 << bit)) for start, piece in pieces]
@@ -109,29 +105,47 @@
     low_table, mats = refs[4:6]
     pieces = refs[6 : 6 + count]
     out = refs[6 + count]
-    basis_r, basis_i, cur_r, cur_i, new_r, new_i, high, low, table, coefs, norms, inner_r, inner_i = refs[7 + count :]
+    basis_r, basis_i, cur_r, cur_i, new_r, new_i, high, low, table, coefs, norms, inner_r, inner_i, staged, arrived = refs[7 + count :]
     rows_total = new_r.shape[0]
     groups = rows_total // 8
     rows_out = out.shape[0] // 2
     zero = jnp.zeros(TILE, jnp.float32)
     dot = functools.partial(jnp.dot, preferred_element_type=jnp.float32)
 
-    for start, piece in zip(starts, pieces):
-
-        def take(g, carry, start=start, piece=piece):
+    copies = []
+    for i, (start, piece) in enumerate(zip(starts, pieces)):
+        into = staged.at[pl.ds(2 * start, piece.shape[0]), :]
+        copies.append(pltpu.make_async_copy(piece, into, arrived.at[i]))
+        copies[-1].start()
+
+    def clear(t, carry):
+        at = pl.ds(pl.multiple_of(t * 8, 8), 8)
+        for ref in (cur_r, cur_i, basis_r.at[0], basis_i.at[0]):
+            ref[at, :] = zero
+        return carry
+
+    lax.fori_loop(0, groups, clear, 0, unroll=8)
+
+    for start, piece, copy in zip(starts, pieces, copies):
+        copy.wait()
+
+        def take(g, carry, start=start):
             row = pl.multiple_of(start + g * 8, 8)
-            new_r[pl.ds(row, 8), :] = piece[pl.ds(pl.multiple_of(g * 16, 16), 8, stride=2), :]
-            new_i[pl.ds(row, 8), :] = piece[pl.ds(g * 16 + 1, 8, stride=2), :]
+            new_r[pl.ds(row, 8), :] = staged[pl.ds(pl.multiple_of(2 * start + g * 16, 16), 8, stride=2), :]
+            new_i[pl.ds(row, 8), :] = staged[pl.ds(2 * start + g * 16 + 1, 8, stride=2), :]
             return carry
 
         lax.fori_loop(0, piece.shape[0] // 16, take, 0, unroll=8)
 
     def block_flips(c):
         base = pl.multiple_of(c * CHUNK, CHUNK)
+        both = mats[0:2].reshape(2 * BLOCK, BLOCK)
         for part, ref in ((0, new_r), (1, new_i)):
             xh, xl = high[part, c], low[part, c]
-            y = dot(mats[0], xh) + dot(mats[1], xh) + dot(mats[0], xl)
-            y = y + dot(xh, mats[2]) + dot(xh, mats[3]) + dot(xl, mats[2])
+            z = dot(both, xh)
+            y = z[:BLOCK] + z[BLOCK:] + dot(mats[0], xl)
+            z = dot(jnp.concatenate([xh, xl]), mats[2])
+            y = y + z[:BLOCK] + z[BLOCK:] + dot(xh, mats[3])
             ref[pl.ds(base, BLOCK), :] = y[:, :LANES]
             ref[pl.ds(base + BLOCK, BLOCK), :] = y[:, LANES:]
 
@@ -148,14 +162,6 @@
     ones = jnp.ones(TILE, jnp.float32)
     for i, value in enumerate((ones, zero, zero, zero)):
         coefs[i] = value
-
-    def clear(t, carry):
-        at = pl.ds(pl.multiple_of(t * 8, 8), 8)
-        for ref in (cur_r, cur_i, basis_r.at[0], basis_i.at[0]):
-            ref[at, :] = zero
-        return carry
-
-    lax.fori_loop(0, groups, clear, 0, unroll=8)
 
     def one_step(step):
         earlier = jnp.maximum(step - 2, 0)
@@ -209,44 +215,46 @@
         norms[step] = total(lax.fori_loop(0, rows_total // span, make, zero))
 
     def products(step):
-        count_rows = 32 if step < 2 else 16 if step < 5 else 8
+        count_rows = 32 if step < 3 else 16
 
         def apply(t, accs):
             base = pl.multiple_of(t * (8 * count_rows), 8 * count_rows)
             at = [pl.ds(pl.multiple_of(base + 8 * r, 8), 8) for r in range(count_rows)]
-            w = []
-            for r in range(count_rows):
-                wr, wi = new_r[at[r], :], new_i[at[r], :]
-                for bit, weight in far:
-                    other = pl.ds(pl.multiple_of((base ^ (1 << bit)) + 8 * r, 8), 8)
-                    wr = wr - weight * cur_r[other, :]
-                    wi = wi - weight * cur_i[other, :]
-                if step + 1 < KRYLOV:
-                    new_r[at[r], :] = wr
-                    new_i[at[r], :] = wi
-                w.append((wr, wi))
             accs = list(accs)
-            for k in range(step + 1):
-                re, im = [], []
-                for r in range(count_rows):
-                    if k == step:
-                        ur, ui = cur_r[at[r], :], cur_i[at[r], :]
-                        basis_r[k, at[r], :] = ur
-                        basis_i[k, at[r], :] = ui
-                    else:
-                        ur, ui = basis_r[k, at[r], :], basis_i[k, at[r], :]
-                    wr, wi = w[r]
-                    re.append(ur * wr + ui * wi)
-                    im.append(ur * wi - ui * wr)
-                    if len(re) == 4:
-                        accs[2 * k] = accs[2 * k] + ((re[0] + re[1]) + (re[2] + re[3]))
-                        accs[2 * k + 1] = accs[2 * k + 1] + ((im[0] + im[1]) + (im[2] + im[3]))
-                        re, im = [], []
+            for first in range(0, count_rows, 4):
+                w = []
+                for r in range(first, first + 4):
+                    wr, wi = new_r[at[r], :], new_i[at[r], :]
+                    for bit, weight in far:
+                        other = pl.ds(pl.multiple_of((base ^ (1 << bit)) + 8 * r, 8), 8)
+                        wr = wr - weight * cur_r[other, :]
+                        wi = wi - weight * cur_i[other, :]
+                    if step + 1 < KRYLOV:
+                        new_r[at[r], :] = wr
+                        new_i[at[r], :] = wi
+                    w.append((wr, wi, wr + wi))
+                for k in range(step + 1):
+                    found = []
+                    for r in range(first, first + 4):
+                        if k == step:
+                            ur, ui = cur_r[at[r], :], cur_i[at[r], :]
+                            basis_r[k, at[r], :] = ur
+                            basis_i[k, at[r], :] = ui
+                        else:
+                            ur, ui = basis_r[k, at[r], :], basis_i[k, at[r], :]
+                        wr, wi, ws = w[r - first]
+                        found.append((ur * wr, ui * wi, (ur - ui) * ws))
+                    for part in range(3):
+                        x = [f[part] for f in found]
+                        accs[3 * k + part] = accs[3 * k + part] + ((x[0] + x[1]) + (x[2] + x[3]))
             return tuple(accs)
 
-        sums = lax.fori_loop(0, groups // count_rows, apply, (zero,) * (2 * step + 2))
+        sums = lax.fori_loop(0, groups // count_rows, apply, (zero,) * (3 * step + 3))
         unit = lax.rsqrt(norms[0]) if step == 0 else ones
-        found = [total(x) * unit for x in sums]
+        found = []
+        for k in range(step + 1):
+            rr, ii, mixed = sums[3 * k : 3 * k + 3]
+            found += [total(rr + ii) * unit, total(mixed - rr + ii) * unit]
         for k in range(step + 1):
             inner_r[step * KRYLOV + k] = found[2 * k]
             inner_i[step * KRYLOV + k] = found[2 * k + 1]
@@ -349,7 +357,8 @@
     weights = []
     for k in range(KRYLOV):
         c = size[0] * inv[k]
-        weights.append((splat(table[k : k + 1, 0:1]) * c, splat(table[k + 8 : k + 9, 0:1]) * c))
+        cr, ci = splat(table[k : k + 1, 0:1]) * c, splat(table[k + 8 : k + 9, 0:1]) * c
+        weights.append((cr, ci - cr, cr + ci))
 
     jump = channel[0]
     first = device[0]
@@ -367,12 +376,14 @@
         for r in range(4):
             g = c * 4 + r
             at = pl.ds(pl.multiple_of(g * 8, 8), 8)
-            pr, pi = zero, zero
+            s1, s2, s3 = zero, zero, zero
             for k in range(KRYLOV):
-                cr, ci = weights[k]
+                cr, less, more = weights[k]
                 ur, ui = basis_r[k, at, :], basis_i[k, at, :]
-                pr = pr + (cr * ur - ci * ui)
-                pi = pi + (cr * ui + ci * ur)
+                s1 = s1 + cr * (ur + ui)
+                s2 = s2 + less * ur
+                s3 = s3 + more * ui
+            pr, pi = s1 - s3, s1 + s2
             new_r[at, :] = pr
             new_i[at, :] = pi
             raised = jnp.where(far_jump, ((g ^ absolute) >> high_bit) & 1, 1)
@@ -461,7 +472,7 @@
     result = pl.pallas_call(
         functools.partial(kernel, spins, [start for start, _ in pieces]),
         out_shape=jax.ShapeDtypeStruct((2 * local_len // LANES, LANES), jnp.float32),
-        in_specs=[smem] * 4 + [vmem] * (2 + len(pieces)),
+        in_specs=[smem] * 4 + [vmem] * 2 + [pl.BlockSpec(memory_space=pl.ANY)] * len(pieces),
         out_specs=vmem,
         scratch_shapes=[
             pltpu.VMEM((KRYLOV, rows_total, LANES), jnp.float32),
@@ -477,6 +488,8 @@
             pltpu.VMEM((KRYLOV,) + TILE, jnp.float32),
             pltpu.VMEM((KRYLOV * KRYLOV,) + TILE, jnp.float32),
             pltpu.VMEM((KRYLOV * KRYLOV,) + TILE, jnp.float32),
+            pltpu.VMEM((2 * rows_total, LANES), jnp.float32),
+            pltpu.SemaphoreType.DMA((len(pieces),)),
         ],
         compiler_params=pltpu.CompilerParams(vmem_limit_bytes=60 * 1024 * 1024),
         name="trajectory",

time: 133 us -> 128 us (0.962); the launches traced: 133 us -> 129 us
  waiting for transfers between devices: 30.7 us -> 28.1 us
  Pallas kernels: 91 us -> 88.8 us
    ppermute x4 -> x6, waiting for transfers between devices: 30.7 us -> 28.1 us  [partner(): return lax.ppermute(value, 'amp', [(i, i ^ mask) for i in range(count)])]
    pallas_call x1, Pallas kernels: 89.3 us -> 87.1 us  [body(): pl.pallas_call(functools.partial(kernel, spins, [start for start, _ in pi...]
    ppermute x4 -> x6, starting transfers between devices: 7.72 us -> 8.52 us  [partner(): return lax.ppermute(value, 'amp', [(i, i ^ mask) for i in range(count)])]
  transfers between devices with their start and end apart: 4 -> 6, of which waited for: 3 -> 3; matrix products, arithmetic and copies ran while one was open for 1% -> 0% of each run, Pallas kernels for 1% -> 1%
where the time goes in v3:
time: 128 us; the launch traced here: 129 us
  Pallas kernels  88.8 us (69%)
  waiting for transfers between devices  28.1 us (22%)
  starting transfers between devices  8.52 us (7%)
  local copies, waits for them, and re-layouts  3.21 us (3%)
    pallas_call x1, Pallas kernels, body(): pl.pallas_call(functools.partial(kernel, spins, [start for start, _ in pi...  87.1 us
    ppermute x6, waiting for transfers between devices, partner(): return lax.ppermute(value, 'amp', [(i, i ^ mask) for i in range(count)])  28.1 us
    ppermute x6, starting transfers between devices, partner(): return lax.ppermute(value, 'amp', [(i, i ^ mask) for i in range(count)])  8.52 us
  transfers between devices with their start and end apart: 6, of which 3 were waited for; matrix products, arithmetic and copies ran while one was open for 0% of the time, Pallas kernels for 1%

profile of v3, /device:TPU:0, one launch (start us, length us, event | category | flops | bytes accessed | tf_op | source)
XLA Modules:
  0.0 129.4 jit_solution(1259816622626401011)
XLA Ops:
  0.0 2.2 %fusion = (f32[1,2,65536]{2,1,0:T(2,128)}, f32[1,2,65536]{2,1,0:T(2,128)}) fusion(f32[1,2,131072]{2,1,0:T(2,128)} %param.5), kind=kLoop, calls=%fused_computation | loop fusion | bytes 2097152 | tf_op jit(solution)/shard_map/slice | solution.py:30
  2.2 3.0 %collective-permute-start.3 = (f32[1,2,65536]{2,1,0:T(2,128)}, f32[1,2,65536]{2,1,0:T(2,128)S(1)}, u32[]{:S(2)}, u32[]{:S(2)}) collective-permute-start(f32[1,2,65536]{2,1,0:T(2,128)} %get-tuple-element.11), channel_id=1, source_target_pairs={{0,2},{1,3},{2,0},{3,1},{4,6},{5,7},{6,4},{7,5},{8,10},{9,11},{10,... | collective-permute-start | bytes 1572872 | tf_op jit(solution)/shard_map/ppermute | solution.py:23
  5.2 1.5 %collective-permute-start = (f32[1,2,65536]{2,1,0:T(2,128)}, f32[1,2,65536]{2,1,0:T(2,128)S(1)}, u32[]{:S(2)}, u32[]{:S(2)}) collective-permute-start(f32[1,2,65536]{2,1,0:T(2,128)} %get-tuple-element.12), channel_id=1, source_target_pairs={{0,1},{1,0},{2,3},{3,2},{4,5},{5,4},{6,7},{7,6},{8,9},{9,8},{10,11... | collective-permute-start | bytes 1572872 | tf_op jit(solution)/shard_map/ppermute | solution.py:23
  6.7 0.5 collective-permute-start.1
  7.3 0.0 collective-permute-start.2
  7.3 11.0 %collective-permute-done.3 = f32[1,2,65536]{2,1,0:T(2,128)S(1)} collective-permute-done((f32[1,2,65536]{2,1,0:T(2,128)}, f32[1,2,65536]{2,1,0:T(2,128)S(1)}, u32[]{:S(2)}, u32[]{:S(2)}) %collective-permute-start.3) | collective-permute-done | bytes 524320 | tf_op jit(solution)/shard_map/ppermute | solution.py:23
  18.2 0.0 copy-start
  18.2 2.0 %collective-permute-start.5 = (f32[1,2,65536]{2,1,0:T(2,128)S(1)}, f32[1,2,65536]{2,1,0:T(2,128)S(1)}, u32[]{:S(2)}, u32[]{:S(2)}) collective-permute-start(f32[1,2,65536]{2,1,0:T(2,128)S(1)} %collective-permute-done.3), channel_id=1, source_target_pairs={{0,1},{1,0},{2,3},{3,2},{4,5},{5,4},{6,7},{7,6},{8,9},{9,8},{10,11... | collective-permute-start | bytes 1572872 | tf_op jit(solution)/shard_map/ppermute | solution.py:23
  20.2 0.0 collective-permute-done
  20.2 0.0 copy-start.1
  20.2 1.5 %collective-permute-start.4 = (f32[1,2,65536]{2,1,0:T(2,128)S(1)}, f32[1,2,65536]{2,1,0:T(2,128)S(1)}, u32[]{:S(2)}, u32[]{:S(2)}) collective-permute-start(f32[1,2,65536]{2,1,0:T(2,128)S(1)} %collective-permute-done), channel_id=1, source_target_pairs={{0,2},{1,3},{2,0},{3,1},{4,6},{5,7},{6,4},{7,5},{8,10},{9,11},{10,... | collective-permute-start | bytes 1572872 | tf_op jit(solution)/shard_map/ppermute | solution.py:23
  22.4 1.8 %tables.1 = (bf16[4,256,256]{2,1,0:T(8,128)(2,1)}, f32[32,128]{1,0:T(8,128)}, f32[8,512]{1,0:T(8,128)}) custom-call(f32[18]{0:T(128)} %couplings.1, f32[19]{0:T(128)} %refs_0_.1, f32[19]{0:T(128)} %decays.1, s32[1]{0:T(128)} %bitcast.device), custom_call_target="tpu_custom_call" | custom-call | flops 20000000 | bytes 1000000 | tf_op jit(solution)/shard_map/tables/pallas_call | solution.py:460
  24.2 7.3 %collective-permute-done.1 = f32[1,2,65536]{2,1,0:T(2,128)S(1)} collective-permute-done((f32[1,2,65536]{2,1,0:T(2,128)}, f32[1,2,65536]{2,1,0:T(2,128)S(1)}, u32[]{:S(2)}, u32[]{:S(2)}) %collective-permute-start.1) | collective-permute-done | bytes 524320 | tf_op jit(solution)/shard_map/ppermute | solution.py:23
  31.5 0.0 copy-start.2
  31.5 0.0 collective-permute-done.2
  31.5 9.8 %collective-permute-done.5 = f32[1,2,65536]{2,1,0:T(2,128)S(1)} collective-permute-done((f32[1,2,65536]{2,1,0:T(2,128)S(1)}, f32[1,2,65536]{2,1,0:T(2,128)S(1)}, u32[]{:S(2)}, u32[]{:S(2)}) %collective-permute-start.5) | collective-permute-done | bytes 524320 | tf_op jit(solution)/shard_map/ppermute | solution.py:23
  41.3 0.0 collective-permute-done.4
  41.3 0.0 copy-done
  41.3 0.0 copy-done.1
  41.3 0.0 copy-done.2
  41.3 0.0 copy-done.3
  41.3 0.8 copy-done.4
  42.1 0.2 copy-done.5
  42.3 87.1 %trajectory.1 = f32[2048,128]{1,0:T(8,128)} custom-call(f32[19]{0:T(128)} %refs_0_.1, f32[8,512]{1,0:T(8,128)} %get-tuple-element.8.refs_1_, s32[1]{0:T(128)S(6)} %copy.14.refs_2_, s32[1]{0:T(128)} %bitcast.1.refs_3_, f32[32,128]{1,0:T(8,128)} %get-tuple-element.9.refs_4_, bf16[4,256,256]{2,1,0:T(8,128)(2,1)} %get-tuple-element.10.refs_5_, ...), custom_call_target="tpu_custom_call" | custom-call | tf_op jit(solution)/shard_map/trajectory/pallas_call | solution.py:472
  (3 shorter events, 0.0 us)
Async XLA Ops:
  2.2 16.0 %collective-permute-start.3 = (f32[1,2,65536]{2,1,0:T(2,128)}, f32[1,2,65536]{2,1,0:T(2,128)S(1)}, u32[]{:S(2)}, u32[]{:S(2)}) collective-permute-start(f32[1,2,65536]{2,1,0:T(2,128)} %get-tuple-element.11), channel_id=1, source_target_pairs={{0,2},{1,3},{2,0},{3,1},{4,6},{5,7},{6,4},{7,5},{8,10},{9,11},{10,... | collective-permute-start | bytes 1572872 | tf_op jit(solution)/shard_map/ppermute | solution.py:23
  5.2 15.0 %collective-permute-start = (f32[1,2,65536]{2,1,0:T(2,128)}, f32[1,2,65536]{2,1,0:T(2,128)S(1)}, u32[]{:S(2)}, u32[]{:S(2)}) collective-permute-start(f32[1,2,65536]{2,1,0:T(2,128)} %get-tuple-element.12), channel_id=1, source_target_pairs={{0,1},{1,0},{2,3},{3,2},{4,5},{5,4},{6,7},{7,6},{8,9},{9,8},{10,11... | collective-permute-start | bytes 1572872 | tf_op jit(solution)/shard_map/ppermute | solution.py:23
  6.7 24.7 %collective-permute-start.1 = (f32[1,2,65536]{2,1,0:T(2,128)}, f32[1,2,65536]{2,1,0:T(2,128)S(1)}, u32[]{:S(2)}, u32[]{:S(2)}) collective-permute-start(f32[1,2,65536]{2,1,0:T(2,128)} %get-tuple-element.11), channel_id=1, source_target_pairs={{0,1},{1,0},{2,3},{3,2},{4,5},{5,4},{6,7},{7,6},{8,9},{9,8},{10,11... | collective-permute-start | bytes 1572872 | tf_op jit(solution)/shard_map/ppermute | solution.py:23
  7.3 24.2 %collective-permute-start.2 = (f32[1,2,65536]{2,1,0:T(2,128)}, f32[1,2,65536]{2,1,0:T(2,128)S(1)}, u32[]{:S(2)}, u32[]{:S(2)}) collective-permute-start(f32[1,2,65536]{2,1,0:T(2,128)} %get-tuple-element.12), channel_id=1, source_target_pairs={{0,2},{1,3},{2,0},{3,1},{4,6},{5,7},{6,4},{7,5},{8,10},{9,11},{10,... | collective-permute-start | bytes 1572872 | tf_op jit(solution)/shard_map/ppermute | solution.py:23
  18.2 23.1 %copy-start = (f32[1,2,65536]{2,1,0:T(2,128)}, f32[1,2,65536]{2,1,0:T(2,128)S(1)}, u32[]{:S(2)}) copy-start(f32[1,2,65536]{2,1,0:T(2,128)S(1)} %collective-permute-done.3) | copy-start | bytes 1572868
  18.2 23.1 %collective-permute-start.5 = (f32[1,2,65536]{2,1,0:T(2,128)S(1)}, f32[1,2,65536]{2,1,0:T(2,128)S(1)}, u32[]{:S(2)}, u32[]{:S(2)}) collective-permute-start(f32[1,2,65536]{2,1,0:T(2,128)S(1)} %collective-permute-done.3), channel_id=1, source_target_pairs={{0,1},{1,0},{2,3},{3,2},{4,5},{5,4},{6,7},{7,6},{8,9},{9,8},{10,11... | collective-permute-start | bytes 1572872 | tf_op jit(solution)/shard_map/ppermute | solution.py:23
  20.2 21.1 %copy-start.1 = (f32[1,2,65536]{2,1,0:T(2,128)}, f32[1,2,65536]{2,1,0:T(2,128)S(1)}, u32[]{:S(2)}) copy-start(f32[1,2,65536]{2,1,0:T(2,128)S(1)} %collective-permute-done) | copy-start | bytes 1572868
  20.2 21.1 %collective-permute-start.4 = (f32[1,2,65536]{2,1,0:T(2,128)S(1)}, f32[1,2,65536]{2,1,0:T(2,128)S(1)}, u32[]{:S(2)}, u32[]{:S(2)}) collective-permute-start(f32[1,2,65536]{2,1,0:T(2,128)S(1)} %collective-permute-done), channel_id=1, source_target_pairs={{0,2},{1,3},{2,0},{3,1},{4,6},{5,7},{6,4},{7,5},{8,10},{9,11},{10,... | collective-permute-start | bytes 1572872 | tf_op jit(solution)/shard_map/ppermute | solution.py:23
  31.5 9.9 %copy-start.2 = (f32[1,2,65536]{2,1,0:T(2,128)}, f32[1,2,65536]{2,1,0:T(2,128)S(1)}, u32[]{:S(2)}) copy-start(f32[1,2,65536]{2,1,0:T(2,128)S(1)} %collective-permute-done.1) | copy-start | bytes 1572868
  31.5 9.9 %copy-start.3 = (f32[1,2,65536]{2,1,0:T(2,128)}, f32[1,2,65536]{2,1,0:T(2,128)S(1)}, u32[]{:S(2)}) copy-start(f32[1,2,65536]{2,1,0:T(2,128)S(1)} %collective-permute-done.2) | copy-start | bytes 1572868
  41.3 0.8 copy-start.4
  41.3 1.0 copy-start.5

commit v4 on v3

--- a/solution.py
+++ b/solution.py
@@ -15,7 +15,7 @@
 TILE = (8, LANES)
 BLOCK = 256
 CHUNK = 2 * BLOCK
-SET_BITS = 2
+SET_BITS = 3
 
 
 def partner(value, mask):

time: 128 us -> 125 us (0.977); the launches traced: 129 us -> 124 us
  Pallas kernels: 88.8 us -> 83.4 us
    pallas_call x1, Pallas kernels: 87.1 us -> 81.6 us  [body(): pl.pallas_call(functools.partial(kernel, spins, [start for start, _ in pi...]
where the time goes in v4:
time: 125 us; the launch traced here: 124 us
  Pallas kernels  83.4 us (67%)
  waiting for transfers between devices  28.1 us (22%)
  starting transfers between devices  8.52 us (7%)
  local copies, waits for them, and re-layouts  3.21 us (3%)
    pallas_call x1, Pallas kernels, body(): pl.pallas_call(functools.partial(kernel, spins, [start for start, _ in pi...  81.6 us
    ppermute x6, waiting for transfers between devices, partner(): return lax.ppermute(value, 'amp', [(i, i ^ mask) for i in range(count)])  28.1 us
    ppermute x6, starting transfers between devices, partner(): return lax.ppermute(value, 'amp', [(i, i ^ mask) for i in range(count)])  8.52 us
  transfers between devices with their start and end apart: 6, of which 3 were waited for; matrix products, arithmetic and copies ran while one was open for 0% of the time, Pallas kernels for 1%

profile of v4, /device:TPU:0, one launch (start us, length us, event | category | flops | bytes accessed | tf_op | source)
XLA Modules:
  0.0 123.9 jit_solution(18143725893153084408)
XLA Ops:
  0.0 2.2 %fusion = (f32[1,2,65536]{2,1,0:T(2,128)}, f32[1,2,65536]{2,1,0:T(2,128)}) fusion(f32[1,2,131072]{2,1,0:T(2,128)} %param.5), kind=kLoop, calls=%fused_computation | loop fusion | bytes 2097152 | tf_op jit(solution)/shard_map/slice | solution.py:30
  2.2 3.0 %collective-permute-start.3 = (f32[1,2,65536]{2,1,0:T(2,128)}, f32[1,2,65536]{2,1,0:T(2,128)S(1)}, u32[]{:S(2)}, u32[]{:S(2)}) collective-permute-start(f32[1,2,65536]{2,1,0:T(2,128)} %get-tuple-element.11), channel_id=1, source_target_pairs={{0,2},{1,3},{2,0},{3,1},{4,6},{5,7},{6,4},{7,5},{8,10},{9,11},{10,... | collective-permute-start | bytes 1572872 | tf_op jit(solution)/shard_map/ppermute | solution.py:23
  5.2 1.5 %collective-permute-start = (f32[1,2,65536]{2,1,0:T(2,128)}, f32[1,2,65536]{2,1,0:T(2,128)S(1)}, u32[]{:S(2)}, u32[]{:S(2)}) collective-permute-start(f32[1,2,65536]{2,1,0:T(2,128)} %get-tuple-element.12), channel_id=1, source_target_pairs={{0,1},{1,0},{2,3},{3,2},{4,5},{5,4},{6,7},{7,6},{8,9},{9,8},{10,11... | collective-permute-start | bytes 1572872 | tf_op jit(solution)/shard_map/ppermute | solution.py:23
  6.7 0.5 collective-permute-start.1
  7.3 0.0 collective-permute-start.2
  7.3 11.0 %collective-permute-done.3 = f32[1,2,65536]{2,1,0:T(2,128)S(1)} collective-permute-done((f32[1,2,65536]{2,1,0:T(2,128)}, f32[1,2,65536]{2,1,0:T(2,128)S(1)}, u32[]{:S(2)}, u32[]{:S(2)}) %collective-permute-start.3) | collective-permute-done | bytes 524320 | tf_op jit(solution)/shard_map/ppermute | solution.py:23
  18.2 0.0 copy-start
  18.2 2.0 %collective-permute-start.5 = (f32[1,2,65536]{2,1,0:T(2,128)S(1)}, f32[1,2,65536]{2,1,0:T(2,128)S(1)}, u32[]{:S(2)}, u32[]{:S(2)}) collective-permute-start(f32[1,2,65536]{2,1,0:T(2,128)S(1)} %collective-permute-done.3), channel_id=1, source_target_pairs={{0,1},{1,0},{2,3},{3,2},{4,5},{5,4},{6,7},{7,6},{8,9},{9,8},{10,11... | collective-permute-start | bytes 1572872 | tf_op jit(solution)/shard_map/ppermute | solution.py:23
  20.2 0.0 collective-permute-done
  20.2 0.0 copy-start.1
  20.2 1.5 %collective-permute-start.4 = (f32[1,2,65536]{2,1,0:T(2,128)S(1)}, f32[1,2,65536]{2,1,0:T(2,128)S(1)}, u32[]{:S(2)}, u32[]{:S(2)}) collective-permute-start(f32[1,2,65536]{2,1,0:T(2,128)S(1)} %collective-permute-done), channel_id=1, source_target_pairs={{0,2},{1,3},{2,0},{3,1},{4,6},{5,7},{6,4},{7,5},{8,10},{9,11},{10,... | collective-permute-start | bytes 1572872 | tf_op jit(solution)/shard_map/ppermute | solution.py:23
  22.4 1.8 %tables.1 = (bf16[4,256,256]{2,1,0:T(8,128)(2,1)}, f32[32,128]{1,0:T(8,128)}, f32[8,512]{1,0:T(8,128)}) custom-call(f32[18]{0:T(128)} %couplings.1, f32[19]{0:T(128)} %refs_0_.1, f32[19]{0:T(128)} %decays.1, s32[1]{0:T(128)} %bitcast.device), custom_call_target="tpu_custom_call" | custom-call | flops 20000000 | bytes 1000000 | tf_op jit(solution)/shard_map/tables/pallas_call | solution.py:460
  24.2 7.3 %collective-permute-done.1 = f32[1,2,65536]{2,1,0:T(2,128)S(1)} collective-permute-done((f32[1,2,65536]{2,1,0:T(2,128)}, f32[1,2,65536]{2,1,0:T(2,128)S(1)}, u32[]{:S(2)}, u32[]{:S(2)}) %collective-permute-start.1) | collective-permute-done | bytes 524320 | tf_op jit(solution)/shard_map/ppermute | solution.py:23
  31.5 0.0 copy-start.2
  31.5 0.0 collective-permute-done.2
  31.5 9.8 %collective-permute-done.5 = f32[1,2,65536]{2,1,0:T(2,128)S(1)} collective-permute-done((f32[1,2,65536]{2,1,0:T(2,128)S(1)}, f32[1,2,65536]{2,1,0:T(2,128)S(1)}, u32[]{:S(2)}, u32[]{:S(2)}) %collective-permute-start.5) | collective-permute-done | bytes 524320 | tf_op jit(solution)/shard_map/ppermute | solution.py:23
  41.3 0.0 collective-permute-done.4
  41.3 0.0 copy-done
  41.3 0.0 copy-done.1
  41.3 0.0 copy-done.2
  41.3 0.0 copy-done.3
  41.3 0.8 copy-done.4
  42.1 0.2 copy-done.5
  42.3 81.6 %trajectory.1 = f32[2048,128]{1,0:T(8,128)} custom-call(f32[19]{0:T(128)} %refs_0_.1, f32[8,512]{1,0:T(8,128)} %get-tuple-element.8.refs_1_, s32[1]{0:T(128)S(6)} %copy.14.refs_2_, s32[1]{0:T(128)} %bitcast.1.refs_3_, f32[32,128]{1,0:T(8,128)} %get-tuple-element.9.refs_4_, bf16[4,256,256]{2,1,0:T(8,128)(2,1)} %get-tuple-element.10.refs_5_, ...), custom_call_target="tpu_custom_call" | custom-call | tf_op jit(solution)/shard_map/trajectory/pallas_call | solution.py:472
  (3 shorter events, 0.0 us)
Async XLA Ops:
  2.2 16.0 %collective-permute-start.3 = (f32[1,2,65536]{2,1,0:T(2,128)}, f32[1,2,65536]{2,1,0:T(2,128)S(1)}, u32[]{:S(2)}, u32[]{:S(2)}) collective-permute-start(f32[1,2,65536]{2,1,0:T(2,128)} %get-tuple-element.11), channel_id=1, source_target_pairs={{0,2},{1,3},{2,0},{3,1},{4,6},{5,7},{6,4},{7,5},{8,10},{9,11},{10,... | collective-permute-start | bytes 1572872 | tf_op jit(solution)/shard_map/ppermute | solution.py:23
  5.2 15.0 %collective-permute-start = (f32[1,2,65536]{2,1,0:T(2,128)}, f32[1,2,65536]{2,1,0:T(2,128)S(1)}, u32[]{:S(2)}, u32[]{:S(2)}) collective-permute-start(f32[1,2,65536]{2,1,0:T(2,128)} %get-tuple-element.12), channel_id=1, source_target_pairs={{0,1},{1,0},{2,3},{3,2},{4,5},{5,4},{6,7},{7,6},{8,9},{9,8},{10,11... | collective-permute-start | bytes 1572872 | tf_op jit(solution)/shard_map/ppermute | solution.py:23
  6.7 24.7 %collective-permute-start.1 = (f32[1,2,65536]{2,1,0:T(2,128)}, f32[1,2,65536]{2,1,0:T(2,128)S(1)}, u32[]{:S(2)}, u32[]{:S(2)}) collective-permute-start(f32[1,2,65536]{2,1,0:T(2,128)} %get-tuple-element.11), channel_id=1, source_target_pairs={{0,1},{1,0},{2,3},{3,2},{4,5},{5,4},{6,7},{7,6},{8,9},{9,8},{10,11... | collective-permute-start | bytes 1572872 | tf_op jit(solution)/shard_map/ppermute | solution.py:23
  7.3 24.2 %collective-permute-start.2 = (f32[1,2,65536]{2,1,0:T(2,128)}, f32[1,2,65536]{2,1,0:T(2,128)S(1)}, u32[]{:S(2)}, u32[]{:S(2)}) collective-permute-start(f32[1,2,65536]{2,1,0:T(2,128)} %get-tuple-element.12), channel_id=1, source_target_pairs={{0,2},{1,3},{2,0},{3,1},{4,6},{5,7},{6,4},{7,5},{8,10},{9,11},{10,... | collective-permute-start | bytes 1572872 | tf_op jit(solution)/shard_map/ppermute | solution.py:23
  18.2 23.1 %copy-start = (f32[1,2,65536]{2,1,0:T(2,128)}, f32[1,2,65536]{2,1,0:T(2,128)S(1)}, u32[]{:S(2)}) copy-start(f32[1,2,65536]{2,1,0:T(2,128)S(1)} %collective-permute-done.3) | copy-start | bytes 1572868
  18.2 23.1 %collective-permute-start.5 = (f32[1,2,65536]{2,1,0:T(2,128)S(1)}, f32[1,2,65536]{2,1,0:T(2,128)S(1)}, u32[]{:S(2)}, u32[]{:S(2)}) collective-permute-start(f32[1,2,65536]{2,1,0:T(2,128)S(1)} %collective-permute-done.3), channel_id=1, source_target_pairs={{0,1},{1,0},{2,3},{3,2},{4,5},{5,4},{6,7},{7,6},{8,9},{9,8},{10,11... | collective-permute-start | bytes 1572872 | tf_op jit(solution)/shard_map/ppermute | solution.py:23
  20.2 21.1 %copy-start.1 = (f32[1,2,65536]{2,1,0:T(2,128)}, f32[1,2,65536]{2,1,0:T(2,128)S(1)}, u32[]{:S(2)}) copy-start(f32[1,2,65536]{2,1,0:T(2,128)S(1)} %collective-permute-done) | copy-start | bytes 1572868
  20.2 21.1 %collective-permute-start.4 = (f32[1,2,65536]{2,1,0:T(2,128)S(1)}, f32[1,2,65536]{2,1,0:T(2,128)S(1)}, u32[]{:S(2)}, u32[]{:S(2)}) collective-permute-start(f32[1,2,65536]{2,1,0:T(2,128)S(1)} %collective-permute-done), channel_id=1, source_target_pairs={{0,2},{1,3},{2,0},{3,1},{4,6},{5,7},{6,4},{7,5},{8,10},{9,11},{10,... | collective-permute-start | bytes 1572872 | tf_op jit(solution)/shard_map/ppermute | solution.py:23
  31.5 9.9 %copy-start.2 = (f32[1,2,65536]{2,1,0:T(2,128)}, f32[1,2,65536]{2,1,0:T(2,128)S(1)}, u32[]{:S(2)}) copy-start(f32[1,2,65536]{2,1,0:T(2,128)S(1)} %collective-permute-done.1) | copy-start | bytes 1572868
  31.5 9.9 %copy-start.3 = (f32[1,2,65536]{2,1,0:T(2,128)}, f32[1,2,65536]{2,1,0:T(2,128)S(1)}, u32[]{:S(2)}) copy-start(f32[1,2,65536]{2,1,0:T(2,128)S(1)} %collective-permute-done.2) | copy-start | bytes 1572868
  41.3 0.8 copy-start.4
  41.3 1.0 copy-start.5
